TPU v7x, 256 devices: a whole 4x4x8 slice. The times are simulated.
256 devices in a mesh: rep: 2 (over core), dp: 128 (over x, y, z).
Axes of the slice: x: 4, y: 4, z: 8, core: 2. Of those that a mesh axis runs over, the one named last changes fastest.
Arguments:
- x: bfloat16 [256, 2048, 896], P(('rep', 'dp')), parts along dimension 0
- dy: bfloat16 [256, 2048, 896], P(('rep', 'dp')), parts along dimension 0
- w_gate: bfloat16 [2, 896, 2304], replicated
- w_up: bfloat16 [2, 896, 2304], replicated
- w_down: bfloat16 [2, 2304, 896], replicated
- m_w_gate: float32 [2, 896, 2304], replicated
- m_w_up: float32 [2, 896, 2304], replicated
- m_w_down: float32 [2, 2304, 896], replicated
- v_w_gate: float32 [2, 896, 2304], replicated
- v_w_up: float32 [2, 896, 2304], replicated
- v_w_down: float32 [2, 2304, 896], replicated
Outputs:
- output 1: bfloat16 [4, 896, 2304], P('rep'), parts along dimension 0
- output 2: bfloat16 [4, 896, 2304], P('rep'), parts along dimension 0
- output 3: bfloat16 [4, 2304, 896], P('rep'), parts along dimension 0
- output 4: float32 [4, 896, 2304], P('rep'), parts along dimension 0
- output 5: float32 [4, 896, 2304], P('rep'), parts along dimension 0
- output 6: float32 [4, 2304, 896], P('rep'), parts along dimension 0
- output 7: float32 [4, 896, 2304], P('rep'), parts along dimension 0
- output 8: float32 [4, 896, 2304], P('rep'), parts along dimension 0
- output 9: float32 [4, 2304, 896], P('rep'), parts along dimension 0
There are 2 independent parts. A program takes and returns all parts, laid end to end along the dimension named above; an argument that names none is the same for every part.
All inputs are finite; a program needn't handle non-finite values.
Results may differ from a plain program's by a relative error of at most 0.022.
Values are sent between devices in bfloat16 or wider.
A program may use at most 768 MiB of HBM per device.

v0:
```python
import functools

import jax
import jax.numpy as jnp
from jax import lax
from jax.experimental import pallas as pl
from jax.experimental.pallas import tpu as pltpu
from jax.sharding import PartitionSpec as P

BF, F32 = jnp.bfloat16, jnp.float32
MESH = pl.DeviceIdType.MESH
SIZES = {"x": 4, "y": 4, "z": 8}
AXES = ("x", "y", "z")
LANES = 128
SHARD = 128
D, FF, TOKENS = 896, 2304, 2048
PANEL = 256
PANELS = FF // PANEL
LIMIT = 66_900_000
ORDERS = (("z", "x", "y"), ("x", "y", "z"), ("y", "x", "z"))
ROWS = ((48, 48, 32), (48, 32, 48), (32, 48, 48))


def colour(j, c):
    return sum(ROWS[j][:c]), ROWS[j][c]


def here():
    d = lax.axis_index("dp")
    return {"x": d // 32, "y": (d // 8) % 4, "z": d % 8}


def device(at, axis, value):
    at = dict(at, **{axis: value})
    return {"dp": (at["x"] * 4 + at["y"]) * 8 + at["z"]}


def shifted(at, axis, by):
    n = SIZES[axis]
    return (at[axis] + (by % n)) % n


def meet(at):
    barrier = pltpu.get_barrier_semaphore()
    peers = [(axis, by) for axis in AXES for by in range(1, SIZES[axis])]
    for axis, by in peers:
        pl.semaphore_signal(barrier, inc=1, device_id=device(at, axis, shifted(at, axis, by)), device_id_type=MESH)
    pl.semaphore_wait(barrier, len(peers))


def place_of(fixed, half, first, rows):
    place, halved = [], half is None
    for a in AXES:
        if a in fixed:
            place.append(fixed[a])
        elif not halved:
            n = SIZES[a] // 2
            place.append(pl.ds(half * n, n))
            halved = True
        else:
            place.append(slice(None))
    begin, size = first, rows
    if not halved:
        one = (rows // 2 + 15) // 16 * 16
        begin, size = (first, one) if half == 0 else (first + one, rows - one)
    return tuple(place) + (pl.ds(begin, size), slice(None))


RATE, LATENCY, SERVE = 45.0e3, 2.2, 0.3


def bytes_of(j, c, phase, part):
    size = SHARD * SHARD * LANES * 2 * ROWS[j][c] // SHARD
    for axis in ORDERS[c][: phase + 1]:
        size //= SIZES[axis]
    return size * part


def scatter_steps(j, c):
    out = []
    for phase, axis in enumerate(ORDERS[c]):
        for s in range(1, SIZES[axis] // 2 + 1):
            out.append((axis, bytes_of(j, c, phase, 0.5 if s == 1 else 1)))
    return out


def gather_steps(j, c):
    out = []
    for phase, axis in reversed(list(enumerate(ORDERS[c]))):
        h = SIZES[axis] // 2
        for s in range(1, h + 1):
            out.append((axis, 2 * bytes_of(j, c, phase, 0.5 if s == h else 1)))
    return out


def serve_order(streams, ready, panels, panel_time):
    free = {axis: 0.0 for axis in AXES}
    arrival, position = {}, {}
    now, done, out = 0.0, 0, []
    waiting = list(streams)

    def send(key, at):
        axis, size = streams[key][at]
        free[axis] = max(now, free[axis]) + size / RATE
        arrival[key], position[key] = free[axis] + LATENCY, at

    while waiting or arrival or done < panels:
        choices = sorted((t, key) for key, t in arrival.items())
        start = next((key for key in waiting if ready[key] <= done and free[streams[key][0][0]] < now + 3.0), None)
        if start is not None:
            now += SERVE
            out.append((now, start))
            waiting.remove(start)
            send(start, 0)
        elif choices and choices[0][0] <= now:
            key = choices[0][1]
            now += SERVE
            out.append((now, key))
            del arrival[key]
            if position[key] + 1 < len(streams[key]):
                send(key, position[key] + 1)
        elif done < panels:
            now += panel_time
            out.append((now, done))
            done += 1
        else:
            later = [choices[0][0]] if choices else []
            later += [free[streams[key][0][0]] - 3.0 for key in waiting]
            now = max(now + 0.01, min(later))
    return out


TB = 256


def dot(a, b):
    return lax.dot_general(a, b, (((1,), (0,)), ((), ())), preferred_element_type=F32)


def dot_t(a, b):
    return lax.dot_general(a, b, (((1,), (1,)), ((), ())), preferred_element_type=F32)


def rows_kernel(x_ref, dy_ref, wg_ref, wu_ref, wd_ref, xt_ref, ys_ref, wg, wu, wd, gate0, up0, a_buf, h_buf, load_sem):
    first = pl.program_id(0) == 0
    loads = {
        (name, layer): pltpu.make_async_copy(ref.at[layer], buf.at[layer], load_sem.at[n, layer])
        for n, (name, ref, buf) in enumerate((("g", wg_ref, wg), ("u", wu_ref, wu), ("d", wd_ref, wd)))
        for layer in range(2)
    }

    @pl.when(first)
    def _():
        for layer in range(2):
            for name in "gud":
                loads[name, layer].start()

    def need(*which):
        @pl.when(first)
        def _():
            for one in which:
                loads[one].wait()

    def scale_of(wide):
        return lax.rsqrt(jnp.mean(wide * wide, -1, keepdims=True) + 1e-6)

    x = x_ref[...].astype(F32)
    a0 = (x * scale_of(x)).astype(BF)
    a_buf[...] = a0
    xt_ref[1, 1] = a0.T
    xt_ref[0, 0] = dy_ref[...].T
    need(("g", 0), ("u", 0))

    def panels(body):
        lax.fori_loop(0, PANELS // 3, lambda i, carry: (body(3 * i), body(3 * i + 1), body(3 * i + 2), carry)[3], 0)

    def at(p):
        return pl.ds(pl.multiple_of(p * PANEL, PANEL), PANEL)

    def forward0(p):
        gate, up = dot(a_buf[...], wg[0, :, at(p)]), dot(a_buf[...], wu[0, :, at(p)])
        gate0[:, at(p)], up0[:, at(p)] = gate, up
        ys_ref[1, 0, :, at(p)] = (gate * lax.logistic(gate) * up).astype(BF)

    panels(forward0)
    need(("d", 0))
    h = x + dot(ys_ref[1, 0], wd[0]).astype(BF).astype(F32)
    h = h.astype(BF).astype(F32)
    h_buf[...] = h
    a1 = (h * scale_of(h)).astype(BF)
    a_buf[...] = a1
    xt_ref[0, 1] = a1.T
    need(("g", 1), ("u", 1), ("d", 1))

    def back(d, gate, up):
        d = d.astype(BF).astype(F32)
        s = lax.logistic(gate)
        silu = gate * s
        return (d * up * (s + silu * (1.0 - s))).astype(BF), (d * silu).astype(BF), (silu * up).astype(BF)

    def both1(p):
        gate, up = dot(a_buf[...], wg[1, :, at(p)]), dot(a_buf[...], wu[1, :, at(p)])
        d = dot_t(dy_ref[...], wd[1, at(p), :])
        ys_ref[0, 1, :, at(p)], ys_ref[0, 2, :, at(p)], ys_ref[0, 0, :, at(p)] = back(d, gate, up)

    panels(both1)
    da = dot_t(ys_ref[0, 1], wg[1]).astype(BF).astype(F32) + dot_t(ys_ref[0, 2], wu[1]).astype(BF).astype(F32)
    da = da.astype(BF).astype(F32)
    h = h_buf[...]
    scale = scale_of(h)
    dh = scale * da - h * (scale * scale * scale * jnp.mean(da * h, -1, keepdims=True))
    dh = (dy_ref[...].astype(F32) + dh.astype(BF).astype(F32)).astype(BF)
    a_buf[...] = dh
    xt_ref[1, 0] = dh.T

    def back0(p):
        d = dot_t(a_buf[...], wd[0, at(p), :])
        ys_ref[1, 1, :, at(p)], ys_ref[1, 2, :, at(p)], _ = back(d, gate0[:, at(p)], up0[:, at(p)])

    panels(back0)


def row_wise(x, dy, w_gate, w_up, w_down):
    tokens = x.shape[0]
    return pl.pallas_call(
        rows_kernel,
        grid=(tokens // TB,),
        out_shape=(jax.ShapeDtypeStruct((2, 2, D, tokens), BF), jax.ShapeDtypeStruct((2, 3, tokens, FF), BF)),
        in_specs=[pl.BlockSpec((TB, D), lambda i: (i, 0))] * 2 + [pl.BlockSpec(memory_space=pltpu.HBM)] * 3,
        out_specs=[
            pl.BlockSpec((2, 2, D, TB), lambda i: (0, 0, 0, i)),
            pl.BlockSpec((2, 3, TB, FF), lambda i: (0, 0, i, 0)),
        ],
        scratch_shapes=[
            pltpu.VMEM((2, D, FF), BF),
            pltpu.VMEM((2, D, FF), BF),
            pltpu.VMEM((2, FF, D), BF),
            pltpu.VMEM((TB, FF), F32),
            pltpu.VMEM((TB, FF), F32),
            pltpu.VMEM((TB, D), BF),
            pltpu.VMEM((TB, D), F32),
            pltpu.SemaphoreType.DMA((3, 2)),
        ],
        compiler_params=pltpu.CompilerParams(vmem_limit_bytes=LIMIT, dimension_semantics=("arbitrary",)),
        cost_estimate=pl.CostEstimate(flops=9 * 2 * tokens * D * FF, bytes_accessed=100_000_000, transcendentals=0),
        name="rows",
    )(x, dy, w_gate, w_up, w_down)


def scatter_actions(j, c, at, own, recv, send_sem, recv_sem, finish):
    first, rows = colour(j, c)
    axes = ORDERS[c]

    def add(target, buffers):
        def body(i, carry):
            place = (...,) if i is None else (i,)
            value = target[place].astype(F32)
            for b in buffers:
                value = value + b[place].astype(F32)
            target[place] = value.astype(BF)
            return carry

        if len(target.shape) == 4:
            lax.fori_loop(0, target.shape[0], body, 0)
        else:
            body(None, 0)

    def parts(phase):
        axis = axes[phase]
        h = SIZES[axis] // 2
        fixed = {a: at[a] for a in axes[:phase]}
        buffer = recv[(j * 3 + c) * 3 + phase]
        base = sum(SIZES[a] // 2 for a in axes[:phase])

        def owner(by):
            return dict(fixed, **{axis: shifted(at, axis, by)})

        def slot(s, d):
            index = owner(0)
            if s > 1:
                return (2 * s - 3 + d,)
            place = place_of(index, d, 0, rows)
            return (0,) + tuple(one for a, one in zip(AXES, place[:3], strict=True) if a not in index) + place[3:]

        def copy(g, s, d):
            sign = (1, -1)[d]
            return pltpu.make_async_remote_copy(
                src_ref=own.at[(g, j, *place_of(owner((h - s + 1) * sign), d if s == 1 else None, first, rows))],
                dst_ref=buffer.at[(g, *slot(s, d))],
                send_sem=send_sem.at[g, j, c, d],
                recv_sem=recv_sem.at[g, j, c, base + s - 1, d],
                device_id=device(at, axis, shifted(at, axis, sign)),
                device_id_type=MESH,
            )

        def step(g, s):
            for d in range(2):
                copy(g, s, d).wait_recv()
            if s < h:
                for d in range(2):
                    by = (h - s) * (1, -1)[d]
                    place = place_of(owner(by), d if s == 1 else None, first, rows)
                    add(own.at[(g, j, *place)], [buffer.at[(g, *slot(s, d))]])
            else:
                place = place_of(owner(0), None, first, rows)
                add(own.at[(g, j, *place)], [buffer.at[(g, *slot(s, d))] for d in range(2)])

        return h, copy, step

    def action(number):
        def run(g):
            left, phase = number, 0
            while phase < 3 and left > SIZES[axes[phase]] // 2:
                left -= SIZES[axes[phase]] // 2
                phase += 1
            h, copy, step = parts(phase)
            if left > 0:
                step(g, left)
            before = [copy(g, left, d) for d in range(2)] if left > 0 else []
            if left == h:
                if phase == 2:
                    for one in before:
                        one.wait_send()
                    finish(g, j, c, own.at[(g, j, *place_of(at, None, first, rows))])
                    return
                _, copy, _ = parts(phase + 1)
                left = 0
            for one in before:
                one.wait_send()
            for d in range(2):
                copy(g, left + 1, d).start()

        return run

    return [action(n) for n in range(1 + sum(SIZES[a] // 2 for a in axes))]


def scatter_order(panel_time=1.15, period=42.0):
    streams = {(j, c): scatter_steps(j, c) for j in range(3) for c in range(3)}
    events = serve_order(streams, {(j, c): PANELS * (j + 1) for j, c in streams}, 3 * PANELS, panel_time)
    panel_ends = [t for t, key in events if not isinstance(key, tuple)]
    slots = [[] for _ in range(len(panel_ends) + 1)]
    count = {key: 0 for key in streams}
    placed = []
    for t, key in events:
        if isinstance(key, tuple):
            placed.append((t % period, int(t // period), key, count[key]))
            count[key] += 1
    for t, late, key, number in sorted(placed):
        slot = sum(end <= t for end in panel_ends) - 1
        slots[max(slot, 0) if slot < len(panel_ends) - 1 or t < panel_ends[-1] + 0.5 else len(panel_ends)].append((late, key, number))
    return slots


def scatter_kernel(xt_ref, ys_ref, shard_ref, squares_ref, own, *refs):
    recv, refs = refs[:27], refs[27:]
    xbuf, ybuf, x_sem, y_sem, send_sem, recv_sem = refs
    at = here()
    total = 3 * PANELS

    def load_x(g, kind):
        return pltpu.make_async_copy(xt_ref.at[g, kind], xbuf.at[kind], x_sem.at[kind])

    def load_y(g, n):
        lanes = pl.ds(pl.multiple_of((n % PANELS) * PANEL, PANEL), PANEL)
        return pltpu.make_async_copy(ys_ref.at[g, n // PANELS, :, lanes], ybuf.at[n % 3], y_sem.at[n % 3])

    load_x(0, 0).start()
    load_y(0, 0).start()
    load_y(0, 1).start()
    load_x(0, 1).start()
    squares_ref[...] = jnp.zeros_like(squares_ref)
    for g in range(2):
        for j in range(3):
            for z in (6, 7):
                own[g, j, 3, 3, z] = jnp.zeros((SHARD, LANES), BF)
    meet(at)

    def finish(g, j, c, region):
        first, rows = colour(j, c)
        value = region[...]
        shard_ref[j, g, pl.ds(first, rows), :] = value
        wide = value.astype(F32)
        squares_ref[...] += jnp.sum((wide * wide).reshape(rows // 8, 8, LANES), axis=0)

    actions = {(j, c): scatter_actions(j, c, at, own, recv, send_sem, recv_sem, finish) for j in range(3) for c in range(3)}
    slots = scatter_order()

    def group(i, carry):
        def slot(n, carry):
            @pl.when(jnp.logical_and(n < total, i < 2))
            def _():
                j, p = n // PANELS, n % PANELS
                kind = jnp.minimum(j, 1)

                @pl.when(n == 0)
                def _():
                    load_x(i, 0).wait()

                @pl.when(n == PANELS)
                def _():
                    load_x(i, 1).wait()

                    @pl.when(i < 1)
                    def _():
                        load_x(i + 1, 0).start()

                load_y(i, n).wait()

                @pl.when(n + 2 < total)
                def _():
                    load_y(i, n + 2).start()

                @pl.when(jnp.logical_and(n + 2 >= total, i < 1))
                def _():
                    load_y(i + 1, n + 2 - total).start()

                out = dot(xbuf[kind], ybuf[n % 3])
                for half in range(PANEL // LANES):
                    for b in range(D // SHARD):
                        d = (2 * p + half) * (D // SHARD) + b
                        block = out[b * SHARD : (b + 1) * SHARD, half * LANES : (half + 1) * LANES]
                        own[i, j, d // 32, (d // 8) % 4, d % 8] = block.astype(BF)

                @pl.when(jnp.logical_and(n == total - 1, i < 1))
                def _():
                    load_x(i + 1, 1).start()

            for number, todo in enumerate(slots):
                if todo:

                    @pl.when(n == number)
                    def _():
                        for late, key, which in todo:

                            @pl.when(i > 0 if late else i < 2)
                            def _():
                                actions[key][which](i - 1 if late else i)

            return carry

        lax.fori_loop(0, total + 1, slot, 0)
        return carry

    lax.fori_loop(0, 3, group, 0)


def recv_shapes():
    shapes = []
    for j in range(3):
        for c in range(3):
            for phase in range(3):
                axes = ORDERS[c]
                left = tuple(SIZES[a] for a in AXES if a not in axes[: phase + 1])
                shapes.append(pltpu.VMEM((2, SIZES[axes[phase]] - 1, *left, ROWS[j][c], LANES), BF))
    return shapes


def scattered(xt, ys):
    sent = 6 * D * FF * 2
    return pl.pallas_call(
        scatter_kernel,
        out_shape=(jax.ShapeDtypeStruct((3, 2, SHARD, LANES), BF), jax.ShapeDtypeStruct((8, LANES), F32)),
        in_specs=[pl.BlockSpec(memory_space=pltpu.HBM)] * 2,
        out_specs=[pl.BlockSpec(memory_space=pltpu.VMEM)] * 2,
        scratch_shapes=[
            pltpu.VMEM((2, 3, 4, 4, 8, SHARD, LANES), BF),
            *recv_shapes(),
            pltpu.VMEM((2, D, TOKENS), BF),
            pltpu.VMEM((3, TOKENS, PANEL), BF),
            pltpu.SemaphoreType.DMA((2,)),
            pltpu.SemaphoreType.DMA((3,)),
            pltpu.SemaphoreType.DMA((2, 3, 3, 2)),
            pltpu.SemaphoreType.DMA((2, 3, 3, 8, 2)),
        ],
        compiler_params=pltpu.CompilerParams(collective_id=0, has_side_effects=True, vmem_limit_bytes=LIMIT),
        cost_estimate=pl.CostEstimate(flops=6 * 2 * TOKENS * D * FF, bytes_accessed=3 * sent, transcendentals=0),
        name="scatter",
    )(xt, ys)


def gather_actions(j, c, at, full, send_sem, recv_sem):
    first, rows = colour(j, c)
    axes = ORDERS[c]
    names = []
    for phase in (2, 1, 0):
        for s in range(1, SIZES[axes[phase]] // 2 + 1):
            names.append((phase, s))

    def copy(number, d):
        phase, s = names[number]
        axis = axes[phase]
        h = SIZES[axis] // 2
        sign = (1, -1)[d]
        index = {a: at[a] for a in axes[:phase]}
        index[axis] = shifted(at, axis, -(s - 1) * sign)
        place = (j, slice(None), *place_of(index, d if s == h else None, first, rows))
        return pltpu.make_async_remote_copy(
            src_ref=full.at[place],
            dst_ref=full.at[place],
            send_sem=send_sem.at[j, c, d],
            recv_sem=recv_sem.at[j, c, number, d],
            device_id=device(at, axis, shifted(at, axis, sign)),
            device_id_type=MESH,
        )

    def arriving(number, d):
        phase, s = names[number]
        axis = axes[phase]
        h = SIZES[axis] // 2
        sign = (1, -1)[d]
        index = {a: at[a] for a in axes[:phase]}
        index[axis] = shifted(at, axis, -s * sign)
        place = (j, slice(None), *place_of(index, d if s == h else None, first, rows))
        return pltpu.make_async_remote_copy(
            src_ref=full.at[place],
            dst_ref=full.at[place],
            send_sem=send_sem.at[j, c, d],
            recv_sem=recv_sem.at[j, c, number, d],
            device_id=device(at, axis, shifted(at, axis, sign)),
            device_id_type=MESH,
        )

    def action(number):
        def run():
            if number > 0:
                for d in range(2):
                    arriving(number - 1, d).wait_recv()
                for d in range(2):
                    copy(number - 1, d).wait_send()
            if number < len(names):
                for d in range(2):
                    copy(number, d).start()

        return run

    return [action(n) for n in range(len(names) + 1)]


def sum_actions(at, squares_ref, total_ref, boxes, send_sem, recv_sem):
    order = ("z", "x", "y")

    def copies(n):
        axis = order[n]
        base = sum(SIZES[a] - 1 for a in order[:n])
        box = boxes[axis]
        return [
            pltpu.make_async_remote_copy(
                src_ref=box.at[at[axis]],
                dst_ref=box.at[at[axis]],
                send_sem=send_sem.at[base + by - 1],
                recv_sem=recv_sem.at[base + by - 1],
                device_id=device(at, axis, shifted(at, axis, by)),
                device_id_type=MESH,
            )
            for by in range(1, SIZES[axis])
        ]

    def action(n):
        def run():
            if n == 0:
                value = squares_ref[...]
            else:
                for one in copies(n - 1):
                    one.wait()
                box = boxes[order[n - 1]]
                value = box[0]
                for i in range(1, SIZES[order[n - 1]]):
                    value = value + box[i]
            if n == len(order):
                total_ref[...] = value
                return
            boxes[order[n]][at[order[n]]] = value
            for one in copies(n):
                one.start()

        return run

    return [action(n) for n in range(len(order) + 1)]


def gather_kernel(shard_ref, squares_ref, out_ref, total_ref, full, box_x, box_y, box_z, load_sem, out_sem, send_sem, recv_sem, sum_send, sum_recv):
    at = here()
    mine = full.at[:, :, at["x"], at["y"], at["z"]]
    load = pltpu.make_async_copy(shard_ref, mine, load_sem)
    load.start()
    meet(at)
    load.wait()
    sums = sum_actions(at, squares_ref, total_ref, {"x": box_x, "y": box_y, "z": box_z}, sum_send, sum_recv)
    sums[0]()
    streams = {(j, c): gather_steps(j, c) for j in range(3) for c in range(3)}
    events = serve_order(streams, dict.fromkeys(streams, 0), 0, 0.0)
    actions = {(j, c): gather_actions(j, c, at, full, send_sem, recv_sem) for j, c in streams}
    count = dict.fromkeys(streams, 0)
    left = {j: 3 for j in range(3)}
    outs = [pltpu.make_async_copy(full.at[j], out_ref.at[j], out_sem.at[j]) for j in range(3)]
    summed = 1
    for t, key in events:
        while summed < len(sums) and t > 5.0 * summed:
            sums[summed]()
            summed += 1
        actions[key][count[key]]()
        count[key] += 1
        if count[key] == len(actions[key]):
            left[key[0]] -= 1
            if left[key[0]] == 0:
                outs[key[0]].start()
    for one in outs:
        one.wait()


def gathered(shards, squares):
    sent = 6 * D * FF * 2
    return pl.pallas_call(
        gather_kernel,
        out_shape=(jax.ShapeDtypeStruct((3, 2, 4, 4, 8, SHARD, LANES), BF), jax.ShapeDtypeStruct((8, LANES), F32)),
        in_specs=[pl.BlockSpec(memory_space=pltpu.HBM), pl.BlockSpec(memory_space=pltpu.VMEM)],
        out_specs=[pl.BlockSpec(memory_space=pltpu.HBM), pl.BlockSpec(memory_space=pltpu.VMEM)],
        scratch_shapes=[
            pltpu.VMEM((3, 2, 4, 4, 8, SHARD, LANES), BF),
            pltpu.VMEM((4, 8, LANES), F32),
            pltpu.VMEM((4, 8, LANES), F32),
            pltpu.VMEM((8, 8, LANES), F32),
            pltpu.SemaphoreType.DMA,
            pltpu.SemaphoreType.DMA((3,)),
            pltpu.SemaphoreType.DMA((3, 3, 2)),
            pltpu.SemaphoreType.DMA((3, 3, 8, 2)),
            pltpu.SemaphoreType.DMA((13,)),
            pltpu.SemaphoreType.DMA((13,)),
        ],
        compiler_params=pltpu.CompilerParams(collective_id=1, has_side_effects=True, vmem_limit_bytes=LIMIT),
        cost_estimate=pl.CostEstimate(flops=sent * 100, bytes_accessed=2 * sent, transcendentals=0),
        name="gather",
    )(shards, squares)


def adamw_kernel(total_ref, g_ref, *refs):
    ins, outs, factor_ref = refs[:9], refs[9:18], refs[18]

    @pl.when(jnp.logical_and(pl.program_id(0) == 0, pl.program_id(1) == 0))
    def _():
        mean = jnp.sum(total_ref[...], keepdims=True) * (1.0 / (6 * D * FF))
        factor_ref[...] = jnp.broadcast_to(jnp.minimum(1.0, 0.5 * lax.rsqrt(mean + 1e-30)), factor_ref.shape)

    factor = factor_ref[0:1, :]

    def one(j, g, place):
        w_ref, m_ref, v_ref = ins[3 * j : 3 * j + 3]
        wo_ref, mo_ref, vo_ref = outs[3 * j : 3 * j + 3]
        w = w_ref[place].astype(F32)
        m = 0.9 * m_ref[place] + 0.1 * g
        v = 0.95 * v_ref[place] + 0.05 * g * g
        step = m * lax.rsqrt(v + 1e-8) + 0.1 * w
        wo_ref[place] = (w - 0.02 * step).astype(BF)
        mo_ref[place] = m
        vo_ref[place] = v

    for half in range(PANEL // LANES):
        lanes = pl.ds(half * LANES, LANES)

        def body(i, carry):
            here_rows = pl.ds(pl.multiple_of(half * D + i * 128, 128), 128)
            rows = pl.ds(pl.multiple_of(i * 128, 128), 128)
            for j in (1, 2):
                one(j, g_ref[j, here_rows, :].astype(F32) * factor, (rows, lanes))
            return carry

        lax.fori_loop(0, D // 128, body, 0)
        for i in range(D // 128):
            g = g_ref[0, pl.ds(half * D + i * 128, 128), :].astype(F32) * factor
            one(0, g.T, (lanes, pl.ds(i * 128, 128)))


def adamw(total, g, weights):
    wide = pl.BlockSpec((None, D, PANEL), lambda l, p: (l, 0, p))
    tall = pl.BlockSpec((None, PANEL, D), lambda l, p: (l, p, 0))
    specs = [tall] * 3 + [wide] * 6
    arrays = [a for one in weights for a in one]
    return pl.pallas_call(
        adamw_kernel,
        grid=(2, PANELS),
        out_shape=[jax.ShapeDtypeStruct(a.shape, a.dtype) for a in arrays],
        in_specs=[
            pl.BlockSpec((8, LANES), lambda l, p: (0, 0)),
            pl.BlockSpec((3, None, PANEL // LANES * D, LANES), lambda l, p: (0, 1 - l, p, 0)),
            *specs,
        ],
        out_specs=specs,
        scratch_shapes=[pltpu.VMEM((8, LANES), F32)],
        compiler_params=pltpu.CompilerParams(vmem_limit_bytes=LIMIT, dimension_semantics=("arbitrary", "arbitrary")),
        cost_estimate=pl.CostEstimate(flops=6 * D * FF * 30, bytes_accessed=6 * D * FF * 22, transcendentals=6 * D * FF),
        name="adamw",
    )(total, g, *arrays)


def solution(mesh):
    def step(x, dy, w_gate, w_up, w_down, m_gate, m_up, m_down, v_gate, v_up, v_down):
        xt, ys = row_wise(x[0], dy[0], w_gate, w_up, w_down)
        shards, squares = scattered(xt, ys)
        full, total = gathered(shards, squares)
        new = adamw(
            total,
            full.reshape(3, 2, 128 * SHARD, LANES),
            ((w_down, m_down, v_down), (w_gate, m_gate, v_gate), (w_up, m_up, v_up)),
        )
        return tuple(new[3 * j + which] for which in range(3) for j in (1, 2, 0))

    return jax.shard_map(
        step,
        mesh=mesh,
        in_specs=(P(("rep", "dp"), None, None),) * 2 + (P(None, None, None),) * 9,
        out_specs=(P("rep", None, None),) * 9,
        check_vma=False,
    )
```

profile of v0, /device:TPU:2, one launch (start us, length us, event | category | flops | bytes accessed | tf_op | source)
XLA Modules:
  0.0 475.2 jit_solution(7834053516056958493)
XLA Ops:
  0.6 124.8 %rows.1 = (bf16[2,2,896,2048]{3,2,1,0:T(8,128)(2,1)}, bf16[2,3,2048,2304]{3,2,1,0:T(8,128)(2,1)}) custom-call(bf16[2048,896]{1,0:T(8,128)(2,1)} %bitcast.4, bf16[2048,896]{1,0:T(8,128)(2,1)} %bitcast.5, bf16[2,896,2304]{2,1,0:T(8,128)(2,1)} %refs_3_.1, bf16[2,896,2304]{2,1,0:T(8,128)(2,1)} %refs_6_.1, bf16[2,2304,896]{2,1,0:T(8,128)(2,1)} %refs_0_.1), custom_call_target="tpu_custom_call" | custom-call | flops 76101451776 | bytes 100000000 | tf_op jit(solution)/shard_map/rows/pallas_call | solution.py:225
  125.5 159.4 %scatter.1 = (bf16[3,2,128,128]{3,2,1,0:T(8,128)(2,1)}, f32[8,128]{1,0:T(8,128)}) custom-call(bf16[2,2,896,2048]{3,2,1,0:T(8,128)(2,1)} %get-tuple-element.24.xt_ref, bf16[2,3,2048,2304]{3,2,1,0:T(8,128)(2,1)} %get-tuple-element.25.ys_ref), custom_call_target="tpu_custom_call" | custom-call | flops 50734301184 | bytes 74317824 | tf_op jit(solution)/shard_map/scatter/pallas_call | solution.py:461
  284.9 100.8 %gather.1 = (bf16[3,2,4,4,8,128,128]{6,5,4,3,2,1,0:T(8,128)(2,1)}, f32[8,128]{1,0:T(8,128)}) custom-call(bf16[3,2,128,128]{3,2,1,0:T(8,128)(2,1)} %get-tuple-element.26.shard_ref, f32[8,128]{1,0:T(8,128)} %get-tuple-element.27.squares_ref), custom_call_target="tpu_custom_call" | custom-call | flops 2477260800 | bytes 49545216 | tf_op jit(solution)/shard_map/gather/pallas_call | solution.py:614
  385.7 89.3 %adamw.1 = (bf16[2,2304,896]{2,1,0:T(8,128)(2,1)}, f32[2,2304,896]{2,1,0:T(8,128)}, f32[2,2304,896]{2,1,0:T(8,128)}, bf16[2,896,2304]{2,1,0:T(8,128)(2,1)}, f32[...) custom-call(f32[8,128]{1,0:T(8,128)} %get-tuple-element.28.total_ref, ...), custom_call_target="tpu_custom_call" | custom-call | flops 371589120 | bytes 272498688 | tf_op jit(solution)/shard_map/adamw/pallas_call | solution.py:679
where the time goes:
time: 475 us
  Pallas kernels  474 us (100%)
    pallas_call x1, Pallas kernels, scattered(): pl.pallas_call(scatter_kernel, out_shape=(jax.ShapeDtypeStruct((3, 2, SHA...  159 us
    pallas_call x1, Pallas kernels, row_wise(): pl.pallas_call(rows_kernel, grid=(tokens // TB,), out_shape=(jax.ShapeDty...  125 us
    pallas_call x1, Pallas kernels, gathered(): pl.pallas_call(gather_kernel, out_shape=(jax.ShapeDtypeStruct((3, 2, 4, 4...  101 us
    pallas_call x1, Pallas kernels, adamw(): pl.pallas_call(adamw_kernel, grid=(2, PANELS), out_shape=[jax.ShapeDtypeS...  89.3 us

commit v1 on v0

--- a/solution.py
+++ b/solution.py
@@ -17,7 +17,7 @@
 PANEL = 256
 PANELS = FF // PANEL
 LIMIT = 66_900_000
-ORDERS = (("z", "x", "y"), ("x", "y", "z"), ("y", "x", "z"))
+ORDERS = tuple((("z", *second), ("x", "y", "z"), ("y", "x", "z")) for second in (("x", "y"), ("y", "x"), ("x", "y")))
 ROWS = ((48, 48, 32), (48, 32, 48), (32, 48, 48))
 
 
@@ -71,32 +71,24 @@
 
 def bytes_of(j, c, phase, part):
     size = SHARD * SHARD * LANES * 2 * ROWS[j][c] // SHARD
-    for axis in ORDERS[c][: phase + 1]:
+    for axis in ORDERS[j][c][: phase + 1]:
         size //= SIZES[axis]
     return size * part
 
 
-def scatter_steps(j, c):
-    out = []
-    for phase, axis in enumerate(ORDERS[c]):
-        for s in range(1, SIZES[axis] // 2 + 1):
-            out.append((axis, bytes_of(j, c, phase, 0.5 if s == 1 else 1)))
-    return out
-
-
 def gather_steps(j, c):
     out = []
-    for phase, axis in reversed(list(enumerate(ORDERS[c]))):
+    for phase, axis in reversed(list(enumerate(ORDERS[j][c]))):
         h = SIZES[axis] // 2
         for s in range(1, h + 1):
             out.append((axis, 2 * bytes_of(j, c, phase, 0.5 if s == h else 1)))
     return out
 
 
-def serve_order(streams, ready, panels, panel_time):
-    free = {axis: 0.0 for axis in AXES}
+def gather_order(streams):
+    free = dict.fromkeys(AXES, 0.0)
     arrival, position = {}, {}
-    now, done, out = 0.0, 0, []
+    now, out = 0.0, []
     waiting = list(streams)
 
     def send(key, at):
@@ -104,9 +96,9 @@
         free[axis] = max(now, free[axis]) + size / RATE
         arrival[key], position[key] = free[axis] + LATENCY, at
 
-    while waiting or arrival or done < panels:
+    while waiting or arrival:
         choices = sorted((t, key) for key, t in arrival.items())
-        start = next((key for key in waiting if ready[key] <= done and free[streams[key][0][0]] < now + 3.0), None)
+        start = next((key for key in waiting if free[streams[key][0][0]] < now + 3.0), None)
         if start is not None:
             now += SERVE
             out.append((now, start))
@@ -119,10 +111,6 @@
             del arrival[key]
             if position[key] + 1 < len(streams[key]):
                 send(key, position[key] + 1)
-        elif done < panels:
-            now += panel_time
-            out.append((now, done))
-            done += 1
         else:
             later = [choices[0][0]] if choices else []
             later += [free[streams[key][0][0]] - 3.0 for key in waiting]
@@ -130,7 +118,7 @@
     return out
 
 
-TB = 256
+TB = 512
 
 
 def dot(a, b):
@@ -141,8 +129,9 @@
     return lax.dot_general(a, b, (((1,), (1,)), ((), ())), preferred_element_type=F32)
 
 
-def rows_kernel(x_ref, dy_ref, wg_ref, wu_ref, wd_ref, xt_ref, ys_ref, wg, wu, wd, gate0, up0, a_buf, h_buf, load_sem):
-    first = pl.program_id(0) == 0
+def rows_kernel(x_ref, dy_ref, wg_ref, wu_ref, wd_ref, xt_hbm, ys_hbm, wg, wu, wd, gate0, up0, a_buf, h_buf, xt_ref, ys_ref, load_sem, xt_sem, ys_sem):
+    block = pl.program_id(0)
+    first, last = block == 0, block == pl.num_programs(0) - 1
     loads = {
         (name, layer): pltpu.make_async_copy(ref.at[layer], buf.at[layer], load_sem.at[n, layer])
         for n, (name, ref, buf) in enumerate((("g", wg_ref, wg), ("u", wu_ref, wu), ("d", wd_ref, wd)))
@@ -161,14 +150,32 @@
             for one in which:
                 loads[one].wait()
 
+    tokens = pl.ds(pl.multiple_of(block * TB, TB), TB)
+
+    def xt_out(*at):
+        return pltpu.make_async_copy(xt_ref.at[at], xt_hbm.at[(*at, slice(None), tokens)], xt_sem.at[at])
+
+    def ys_out(*at):
+        return pltpu.make_async_copy(ys_ref.at[at], ys_hbm.at[(*at, tokens, slice(None))], ys_sem.at[at])
+
+    def free(*outs):
+        @pl.when(jnp.logical_not(first))
+        def _():
+            for one in outs:
+                one.wait()
+
     def scale_of(wide):
         return lax.rsqrt(jnp.mean(wide * wide, -1, keepdims=True) + 1e-6)
 
     x = x_ref[...].astype(F32)
     a0 = (x * scale_of(x)).astype(BF)
     a_buf[...] = a0
+    free(xt_out(1, 1), xt_out(0, 0))
     xt_ref[1, 1] = a0.T
     xt_ref[0, 0] = dy_ref[...].T
+    xt_out(1, 1).start()
+    xt_out(0, 0).start()
+    free(ys_out(1, 0))
     need(("g", 0), ("u", 0))
 
     def panels(body):
@@ -183,13 +190,17 @@
         ys_ref[1, 0, :, at(p)] = (gate * lax.logistic(gate) * up).astype(BF)
 
     panels(forward0)
+    ys_out(1, 0).start()
     need(("d", 0))
     h = x + dot(ys_ref[1, 0], wd[0]).astype(BF).astype(F32)
     h = h.astype(BF).astype(F32)
     h_buf[...] = h
     a1 = (h * scale_of(h)).astype(BF)
     a_buf[...] = a1
+    free(xt_out(0, 1))
     xt_ref[0, 1] = a1.T
+    xt_out(0, 1).start()
+    free(ys_out(0, 0), ys_out(0, 1), ys_out(0, 2))
     need(("g", 1), ("u", 1), ("d", 1))
 
     def back(d, gate, up):
@@ -204,6 +215,8 @@
         ys_ref[0, 1, :, at(p)], ys_ref[0, 2, :, at(p)], ys_ref[0, 0, :, at(p)] = back(d, gate, up)
 
     panels(both1)
+    for j in range(3):
+        ys_out(0, j).start()
     da = dot_t(ys_ref[0, 1], wg[1]).astype(BF).astype(F32) + dot_t(ys_ref[0, 2], wu[1]).astype(BF).astype(F32)
     da = da.astype(BF).astype(F32)
     h = h_buf[...]
@@ -211,13 +224,26 @@
     dh = scale * da - h * (scale * scale * scale * jnp.mean(da * h, -1, keepdims=True))
     dh = (dy_ref[...].astype(F32) + dh.astype(BF).astype(F32)).astype(BF)
     a_buf[...] = dh
+    free(xt_out(1, 0))
     xt_ref[1, 0] = dh.T
+    xt_out(1, 0).start()
+    free(ys_out(1, 1), ys_out(1, 2))
 
     def back0(p):
         d = dot_t(a_buf[...], wd[0, at(p), :])
         ys_ref[1, 1, :, at(p)], ys_ref[1, 2, :, at(p)], _ = back(d, gate0[:, at(p)], up0[:, at(p)])
 
     panels(back0)
+    for j in (1, 2):
+        ys_out(1, j).start()
+
+    @pl.when(last)
+    def _():
+        for g in range(2):
+            for kind in range(2):
+                xt_out(g, kind).wait()
+            for j in range(3):
+                ys_out(g, j).wait()
 
 
 def row_wise(x, dy, w_gate, w_up, w_down):
@@ -227,10 +253,7 @@
         grid=(tokens // TB,),
         out_shape=(jax.ShapeDtypeStruct((2, 2, D, tokens), BF), jax.ShapeDtypeStruct((2, 3, tokens, FF), BF)),
         in_specs=[pl.BlockSpec((TB, D), lambda i: (i, 0))] * 2 + [pl.BlockSpec(memory_space=pltpu.HBM)] * 3,
-        out_specs=[
-            pl.BlockSpec((2, 2, D, TB), lambda i: (0, 0, 0, i)),
-            pl.BlockSpec((2, 3, TB, FF), lambda i: (0, 0, i, 0)),
-        ],
+        out_specs=[pl.BlockSpec(memory_space=pltpu.HBM)] * 2,
         scratch_shapes=[
             pltpu.VMEM((2, D, FF), BF),
             pltpu.VMEM((2, D, FF), BF),
@@ -239,7 +262,11 @@
             pltpu.VMEM((TB, FF), F32),
             pltpu.VMEM((TB, D), BF),
             pltpu.VMEM((TB, D), F32),
+            pltpu.VMEM((2, 2, D, TB), BF),
+            pltpu.VMEM((2, 3, TB, FF), BF),
             pltpu.SemaphoreType.DMA((3, 2)),
+            pltpu.SemaphoreType.DMA((2, 2)),
+            pltpu.SemaphoreType.DMA((2, 3)),
         ],
         compiler_params=pltpu.CompilerParams(vmem_limit_bytes=LIMIT, dimension_semantics=("arbitrary",)),
         cost_estimate=pl.CostEstimate(flops=9 * 2 * tokens * D * FF, bytes_accessed=100_000_000, transcendentals=0),
@@ -249,7 +276,7 @@
 
 def scatter_actions(j, c, at, own, recv, send_sem, recv_sem, finish):
     first, rows = colour(j, c)
-    axes = ORDERS[c]
+    axes = ORDERS[j][c]
 
     def add(target, buffers):
         def body(i, carry):
@@ -335,21 +362,36 @@
     return [action(n) for n in range(1 + sum(SIZES[a] // 2 for a in axes))]
 
 
-def scatter_order(panel_time=1.15, period=42.0):
-    streams = {(j, c): scatter_steps(j, c) for j in range(3) for c in range(3)}
-    events = serve_order(streams, {(j, c): PANELS * (j + 1) for j, c in streams}, 3 * PANELS, panel_time)
-    panel_ends = [t for t, key in events if not isinstance(key, tuple)]
-    slots = [[] for _ in range(len(panel_ends) + 1)]
-    count = {key: 0 for key in streams}
-    placed = []
-    for t, key in events:
-        if isinstance(key, tuple):
-            placed.append((t % period, int(t // period), key, count[key]))
-            count[key] += 1
-    for t, late, key, number in sorted(placed):
-        slot = sum(end <= t for end in panel_ends) - 1
-        slots[max(slot, 0) if slot < len(panel_ends) - 1 or t < panel_ends[-1] + 0.5 else len(panel_ends)].append((late, key, number))
-    return slots
+SLOTS = (
+    ((2, 8, 5),),
+    ((2, 1, 6),),
+    ((1, 7, 1),),
+    (),
+    ((1, 8, 1), (1, 6, 2),),
+    ((2, 2, 6), (1, 3, 2),),
+    ((2, 6, 6),),
+    ((2, 0, 6), (1, 4, 2), (2, 5, 6), (2, 4, 6), (2, 7, 6),),
+    ((0, 1, 0), (0, 0, 0), (0, 2, 0), (1, 5, 2),),
+    ((1, 2, 3),),
+    ((1, 6, 3),),
+    ((1, 0, 4), (2, 8, 6), (2, 3, 6),),
+    (),
+    ((1, 7, 2), (0, 0, 1), (1, 1, 3), (1, 3, 3), (1, 8, 2),),
+    ((2, 1, 7), (0, 1, 1),),
+    ((0, 2, 1),),
+    ((2, 5, 7),),
+    ((0, 5, 0),),
+    ((1, 4, 3), (1, 5, 3),),
+    ((2, 4, 7),),
+    ((0, 3, 0),),
+    ((1, 6, 4), (0, 0, 2), (0, 4, 0),),
+    ((2, 2, 7), (1, 7, 3),),
+    (),
+    ((1, 8, 3),),
+    (),
+    ((2, 0, 7), (2, 6, 7), (2, 7, 7), (0, 8, 0), (0, 6, 0), (2, 8, 7), (1, 2, 4), (1, 6, 5), (0, 7, 0), (1, 4, 4), (1, 1, 4), (0, 1, 2), (0, 3, 1), (1, 5, 4), (1, 3, 4), (2, 3, 7), (1, 0, 5), (0, 5, 1), (2, 1, 8), (2, 5, 8), (1, 7, 4), (0, 2, 2), (1, 8, 4), (0, 6, 1), (2, 4, 8), (1, 1, 5), (1, 2, 5), (2, 0, 8), (2, 2, 8), (0, 4, 1), (2, 6, 8), (1, 5, 5), (2, 7, 8), (0, 0, 3), (1, 4, 5), (1, 3, 5), (2, 8, 8), (1, 7, 5), (2, 3, 8),),
+    (),
+)
 
 
 def scatter_kernel(xt_ref, ys_ref, shard_ref, squares_ref, own, *refs):
@@ -383,8 +425,8 @@
         wide = value.astype(F32)
         squares_ref[...] += jnp.sum((wide * wide).reshape(rows // 8, 8, LANES), axis=0)
 
-    actions = {(j, c): scatter_actions(j, c, at, own, recv, send_sem, recv_sem, finish) for j in range(3) for c in range(3)}
-    slots = scatter_order()
+    actions = [scatter_actions(j, c, at, own, recv, send_sem, recv_sem, finish) for j in range(3) for c in range(3)]
+    rounds = 2 + max(late for todo in SLOTS for late, _, _ in todo)
 
     def group(i, carry):
         def slot(n, carry):
@@ -426,23 +468,19 @@
                 def _():
                     load_x(i + 1, 1).start()
 
-            for number, todo in enumerate(slots):
+            def serve(todo):
+                for late, key, which in todo:
+                    pl.when(jnp.logical_and(i >= late, i < 2 + late))(functools.partial(actions[key][which], i - late))
+
+            for number, todo in enumerate(SLOTS):
                 if todo:
-
-                    @pl.when(n == number)
-                    def _():
-                        for late, key, which in todo:
-
-                            @pl.when(i > 0 if late else i < 2)
-                            def _():
-                                actions[key][which](i - 1 if late else i)
-
+                    pl.when(n == number)(functools.partial(serve, todo))
             return carry
 
         lax.fori_loop(0, total + 1, slot, 0)
         return carry
 
-    lax.fori_loop(0, 3, group, 0)
+    lax.fori_loop(0, rounds, group, 0)
 
 
 def recv_shapes():
@@ -450,7 +488,7 @@
     for j in range(3):
         for c in range(3):
             for phase in range(3):
-                axes = ORDERS[c]
+                axes = ORDERS[j][c]
                 left = tuple(SIZES[a] for a in AXES if a not in axes[: phase + 1])
                 shapes.append(pltpu.VMEM((2, SIZES[axes[phase]] - 1, *left, ROWS[j][c], LANES), BF))
     return shapes
@@ -481,7 +519,7 @@
 
 def gather_actions(j, c, at, full, send_sem, recv_sem):
     first, rows = colour(j, c)
-    axes = ORDERS[c]
+    axes = ORDERS[j][c]
     names = []
     for phase in (2, 1, 0):
         for s in range(1, SIZES[axes[phase]] // 2 + 1):
@@ -589,7 +627,7 @@
     sums = sum_actions(at, squares_ref, total_ref, {"x": box_x, "y": box_y, "z": box_z}, sum_send, sum_recv)
     sums[0]()
     streams = {(j, c): gather_steps(j, c) for j in range(3) for c in range(3)}
-    events = serve_order(streams, dict.fromkeys(streams, 0), 0, 0.0)
+    events = gather_order(streams)
     actions = {(j, c): gather_actions(j, c, at, full, send_sem, recv_sem) for j, c in streams}
     count = dict.fromkeys(streams, 0)
     left = {j: 3 for j in range(3)}

time: 475 us -> 460 us (0.968)
  Pallas kernels: 474 us -> 459 us
    pallas_call x1, Pallas kernels: 159 us -> 149 us  [scattered(): pl.pallas_call(scatter_kernel, out_shape=(jax.ShapeDtypeStruct((3, 2, SHA...]
    pallas_call x1, Pallas kernels: 125 us -> 118 us  [row_wise(): pl.pallas_call(rows_kernel, grid=(tokens // TB,), out_shape=(jax.ShapeDty...]
where the time goes in v1:
time: 460 us; the launch traced here: 459 us
  Pallas kernels  459 us (100%)
    pallas_call x1, Pallas kernels, scattered(): pl.pallas_call(scatter_kernel, out_shape=(jax.ShapeDtypeStruct((3, 2, SHA...  149 us
    pallas_call x1, Pallas kernels, row_wise(): pl.pallas_call(rows_kernel, grid=(tokens // TB,), out_shape=(jax.ShapeDty...  118 us
    pallas_call x1, Pallas kernels, gathered(): pl.pallas_call(gather_kernel, out_shape=(jax.ShapeDtypeStruct((3, 2, 4, 4...  102 us
    pallas_call x1, Pallas kernels, adamw(): pl.pallas_call(adamw_kernel, grid=(2, PANELS), out_shape=[jax.ShapeDtypeS...  89.3 us

profile of v1, /device:TPU:2, one launch (start us, length us, event | category | flops | bytes accessed | tf_op | source)
XLA Modules:
  0.0 459.5 jit_solution(3500116617559177990)
XLA Ops:
  0.6 117.8 %rows.1 = (bf16[2,2,896,2048]{3,2,1,0:T(8,128)(2,1)}, bf16[2,3,2048,2304]{3,2,1,0:T(8,128)(2,1)}) custom-call(bf16[2048,896]{1,0:T(8,128)(2,1)} %bitcast.4, bf16[2048,896]{1,0:T(8,128)(2,1)} %bitcast.5, bf16[2,896,2304]{2,1,0:T(8,128)(2,1)} %refs_3_.1, bf16[2,896,2304]{2,1,0:T(8,128)(2,1)} %refs_6_.1, bf16[2,2304,896]{2,1,0:T(8,128)(2,1)} %refs_0_.1), custom_call_target="tpu_custom_call" | custom-call | flops 76101451776 | bytes 100000000 | tf_op jit(solution)/shard_map/rows/pallas_call | solution.py:251
  118.5 149.2 %scatter.1 = (bf16[3,2,128,128]{3,2,1,0:T(8,128)(2,1)}, f32[8,128]{1,0:T(8,128)}) custom-call(bf16[2,2,896,2048]{3,2,1,0:T(8,128)(2,1)} %get-tuple-element.24.xt_ref, bf16[2,3,2048,2304]{3,2,1,0:T(8,128)(2,1)} %get-tuple-element.25.ys_ref), custom_call_target="tpu_custom_call" | custom-call | flops 50734301184 | bytes 74317824 | tf_op jit(solution)/shard_map/scatter/pallas_call | solution.py:499
  267.7 102.3 %gather.1 = (bf16[3,2,4,4,8,128,128]{6,5,4,3,2,1,0:T(8,128)(2,1)}, f32[8,128]{1,0:T(8,128)}) custom-call(bf16[3,2,128,128]{3,2,1,0:T(8,128)(2,1)} %get-tuple-element.26.shard_ref, f32[8,128]{1,0:T(8,128)} %get-tuple-element.27.squares_ref), custom_call_target="tpu_custom_call" | custom-call | flops 2477260800 | bytes 49545216 | tf_op jit(solution)/shard_map/gather/pallas_call | solution.py:652
  370.0 89.3 %adamw.1 = (bf16[2,2304,896]{2,1,0:T(8,128)(2,1)}, f32[2,2304,896]{2,1,0:T(8,128)}, f32[2,2304,896]{2,1,0:T(8,128)}, bf16[2,896,2304]{2,1,0:T(8,128)(2,1)}, f32[...) custom-call(f32[8,128]{1,0:T(8,128)} %get-tuple-element.28.total_ref, ...), custom_call_target="tpu_custom_call" | custom-call | flops 371589120 | bytes 272498688 | tf_op jit(solution)/shard_map/adamw/pallas_call | solution.py:717

commit v2 on v1

--- a/solution.py
+++ b/solution.py
@@ -66,58 +66,6 @@
     return tuple(place) + (pl.ds(begin, size), slice(None))
 
 
-RATE, LATENCY, SERVE = 45.0e3, 2.2, 0.3
-
-
-def bytes_of(j, c, phase, part):
-    size = SHARD * SHARD * LANES * 2 * ROWS[j][c] // SHARD
-    for axis in ORDERS[j][c][: phase + 1]:
-        size //= SIZES[axis]
-    return size * part
-
-
-def gather_steps(j, c):
-    out = []
-    for phase, axis in reversed(list(enumerate(ORDERS[j][c]))):
-        h = SIZES[axis] // 2
-        for s in range(1, h + 1):
-            out.append((axis, 2 * bytes_of(j, c, phase, 0.5 if s == h else 1)))
-    return out
-
-
-def gather_order(streams):
-    free = dict.fromkeys(AXES, 0.0)
-    arrival, position = {}, {}
-    now, out = 0.0, []
-    waiting = list(streams)
-
-    def send(key, at):
-        axis, size = streams[key][at]
-        free[axis] = max(now, free[axis]) + size / RATE
-        arrival[key], position[key] = free[axis] + LATENCY, at
-
-    while waiting or arrival:
-        choices = sorted((t, key) for key, t in arrival.items())
-        start = next((key for key in waiting if free[streams[key][0][0]] < now + 3.0), None)
-        if start is not None:
-            now += SERVE
-            out.append((now, start))
-            waiting.remove(start)
-            send(start, 0)
-        elif choices and choices[0][0] <= now:
-            key = choices[0][1]
-            now += SERVE
-            out.append((now, key))
-            del arrival[key]
-            if position[key] + 1 < len(streams[key]):
-                send(key, position[key] + 1)
-        else:
-            later = [choices[0][0]] if choices else []
-            later += [free[streams[key][0][0]] - 3.0 for key in waiting]
-            now = max(now + 0.01, min(later))
-    return out
-
-
 TB = 512
 
 
@@ -179,10 +127,11 @@
     need(("g", 0), ("u", 0))
 
     def panels(body):
-        lax.fori_loop(0, PANELS // 3, lambda i, carry: (body(3 * i), body(3 * i + 1), body(3 * i + 2), carry)[3], 0)
+        for p in range(PANELS):
+            body(p)
 
     def at(p):
-        return pl.ds(pl.multiple_of(p * PANEL, PANEL), PANEL)
+        return pl.ds(p * PANEL, PANEL)
 
     def forward0(p):
         gate, up = dot(a_buf[...], wg[0, :, at(p)]), dot(a_buf[...], wu[0, :, at(p)])
@@ -363,33 +312,33 @@
 
 
 SLOTS = (
-    ((2, 8, 5),),
-    ((2, 1, 6),),
-    ((1, 7, 1),),
-    (),
-    ((1, 8, 1), (1, 6, 2),),
-    ((2, 2, 6), (1, 3, 2),),
-    ((2, 6, 6),),
-    ((2, 0, 6), (1, 4, 2), (2, 5, 6), (2, 4, 6), (2, 7, 6),),
-    ((0, 1, 0), (0, 0, 0), (0, 2, 0), (1, 5, 2),),
-    ((1, 2, 3),),
+    (),
+    (),
+    ((1, 1, 3),),
+    ((1, 4, 2),),
+    (),
+    ((1, 6, 2),),
+    (),
+    ((1, 8, 2),),
+    ((1, 0, 4), (0, 1, 0), (0, 2, 0),),
+    ((2, 3, 6), (1, 7, 2),),
+    ((1, 5, 3), (0, 0, 0), (2, 2, 6),),
+    (),
+    ((0, 2, 1), (2, 4, 6),),
+    ((1, 1, 4),),
+    ((2, 5, 6), (0, 0, 1), (2, 6, 6),),
+    ((2, 8, 6), (0, 1, 1),),
+    ((2, 7, 6),),
+    ((2, 0, 7), (0, 5, 0), (0, 3, 0),),
     ((1, 6, 3),),
-    ((1, 0, 4), (2, 8, 6), (2, 3, 6),),
-    (),
-    ((1, 7, 2), (0, 0, 1), (1, 1, 3), (1, 3, 3), (1, 8, 2),),
-    ((2, 1, 7), (0, 1, 1),),
-    ((0, 2, 1),),
-    ((2, 5, 7),),
-    ((0, 5, 0),),
-    ((1, 4, 3), (1, 5, 3),),
-    ((2, 4, 7),),
-    ((0, 3, 0),),
-    ((1, 6, 4), (0, 0, 2), (0, 4, 0),),
-    ((2, 2, 7), (1, 7, 3),),
-    (),
-    ((1, 8, 3),),
-    (),
-    ((2, 0, 7), (2, 6, 7), (2, 7, 7), (0, 8, 0), (0, 6, 0), (2, 8, 7), (1, 2, 4), (1, 6, 5), (0, 7, 0), (1, 4, 4), (1, 1, 4), (0, 1, 2), (0, 3, 1), (1, 5, 4), (1, 3, 4), (2, 3, 7), (1, 0, 5), (0, 5, 1), (2, 1, 8), (2, 5, 8), (1, 7, 4), (0, 2, 2), (1, 8, 4), (0, 6, 1), (2, 4, 8), (1, 1, 5), (1, 2, 5), (2, 0, 8), (2, 2, 8), (0, 4, 1), (2, 6, 8), (1, 5, 5), (2, 7, 8), (0, 0, 3), (1, 4, 5), (1, 3, 5), (2, 8, 8), (1, 7, 5), (2, 3, 8),),
+    ((0, 4, 0), (1, 4, 3), (1, 8, 3),),
+    ((0, 3, 1), (1, 2, 4),),
+    ((0, 5, 1), (0, 0, 2),),
+    (),
+    ((1, 0, 5),),
+    (),
+    (),
+    ((0, 7, 0), (1, 3, 4), (1, 1, 5), (2, 4, 7), (0, 6, 0), (1, 7, 3), (2, 1, 7), (2, 5, 7), (0, 3, 2), (2, 3, 7), (1, 4, 4), (0, 2, 2), (2, 2, 7), (0, 8, 0), (1, 5, 4), (2, 6, 7), (1, 3, 5), (0, 5, 2), (1, 6, 4), (1, 2, 5), (2, 8, 7), (0, 4, 1), (0, 6, 1), (2, 7, 7), (2, 0, 8), (0, 1, 2), (1, 8, 4), (2, 1, 8), (1, 7, 4), (0, 0, 3), (1, 1, 6), (2, 4, 8), (1, 4, 5), (0, 7, 1), (2, 2, 8), (1, 5, 5), (2, 6, 8), (1, 6, 5), (0, 2, 3), (2, 5, 8), (2, 3, 8), (2, 8, 8), (0, 8, 1), (0, 3, 3), (1, 8, 5), (2, 7, 8), (1, 7, 5), (1, 0, 6),),
     (),
 )
 
@@ -472,9 +421,13 @@
                 for late, key, which in todo:
                     pl.when(jnp.logical_and(i >= late, i < 2 + late))(functools.partial(actions[key][which], i - late))
 
-            for number, todo in enumerate(SLOTS):
-                if todo:
-                    pl.when(n == number)(functools.partial(serve, todo))
+            def some(low):
+                for number in range(low, min(low + 5, len(SLOTS))):
+                    if SLOTS[number]:
+                        pl.when(n == number)(functools.partial(serve, SLOTS[number]))
+
+            for low in range(0, len(SLOTS), 5):
+                pl.when(n // 5 == low // 5)(functools.partial(some, low))
             return carry
 
         lax.fori_loop(0, total + 1, slot, 0)
@@ -575,6 +528,13 @@
     return [action(n) for n in range(len(names) + 1)]
 
 
+GATHER = (
+    *(4, 6, 2, 3, 7, 5, 0, 4, 6, 2, 3, 7, 5, 0, 4, 6, 2, 3, 1, 8, 7, 0, 4, 2, 5, 1, 8),
+    *(6, 7, 4, 2, 5, 8, 1, 0, 7, 3, 5, 8, 4, 1, 6, 2, 8, 1, 5, 0, 7, 4, 3, 2, 1, 7, 8),
+    *(5, 0, 1, 2, 6, 3, 8, 5, 7, 6, 3, 0, 6, 1, 0, 2, 4, 3, 8, 6, 3, 5, 7, 0, 1, 8, 4),
+)
+
+
 def sum_actions(at, squares_ref, total_ref, boxes, send_sem, recv_sem):
     order = ("z", "x", "y")
 
@@ -626,23 +586,21 @@
     load.wait()
     sums = sum_actions(at, squares_ref, total_ref, {"x": box_x, "y": box_y, "z": box_z}, sum_send, sum_recv)
     sums[0]()
-    streams = {(j, c): gather_steps(j, c) for j in range(3) for c in range(3)}
-    events = gather_order(streams)
-    actions = {(j, c): gather_actions(j, c, at, full, send_sem, recv_sem) for j, c in streams}
-    count = dict.fromkeys(streams, 0)
+    actions = [gather_actions(j, c, at, full, send_sem, recv_sem) for j in range(3) for c in range(3)]
+    count = [0] * 9
     left = {j: 3 for j in range(3)}
     outs = [pltpu.make_async_copy(full.at[j], out_ref.at[j], out_sem.at[j]) for j in range(3)]
     summed = 1
-    for t, key in events:
-        while summed < len(sums) and t > 5.0 * summed:
+    for number, key in enumerate(GATHER):
+        if number in (18, 24, 30):
             sums[summed]()
             summed += 1
         actions[key][count[key]]()
         count[key] += 1
         if count[key] == len(actions[key]):
-            left[key[0]] -= 1
-            if left[key[0]] == 0:
-                outs[key[0]].start()
+            left[key // 3] -= 1
+            if left[key // 3] == 0:
+                outs[key // 3].start()
     for one in outs:
         one.wait()
 

time: 460 us -> 452 us (0.983)
  Pallas kernels: 459 us -> 452 us
    pallas_call x1, Pallas kernels: 118 us -> 111 us  [row_wise(): pl.pallas_call(rows_kernel, grid=(tokens // TB,), out_shape=(jax.ShapeDty...]
    pallas_call x1, Pallas kernels: 149 us -> 142 us  [scattered(): pl.pallas_call(scatter_kernel, out_shape=(jax.ShapeDtypeStruct((3, 2, SHA...]
    pallas_call x1, Pallas kernels: 102 us -> 109 us  [gathered(): pl.pallas_call(gather_kernel, out_shape=(jax.ShapeDtypeStruct((3, 2, 4, 4...]
where the time goes in v2:
time: 452 us
  Pallas kernels  452 us (100%)
    pallas_call x1, Pallas kernels, scattered(): pl.pallas_call(scatter_kernel, out_shape=(jax.ShapeDtypeStruct((3, 2, SHA...  142 us
    pallas_call x1, Pallas kernels, row_wise(): pl.pallas_call(rows_kernel, grid=(tokens // TB,), out_shape=(jax.ShapeDty...  111 us
    pallas_call x1, Pallas kernels, gathered(): pl.pallas_call(gather_kernel, out_shape=(jax.ShapeDtypeStruct((3, 2, 4, 4...  109 us
    pallas_call x1, Pallas kernels, adamw(): pl.pallas_call(adamw_kernel, grid=(2, PANELS), out_shape=[jax.ShapeDtypeS...  89.3 us

profile of v2, /device:TPU:2, one launch (start us, length us, event | category | flops | bytes accessed | tf_op | source)
XLA Modules:
  0.0 452.3 jit_solution(343256766671177477)
XLA Ops:
  0.6 110.7 %rows.1 = (bf16[2,2,896,2048]{3,2,1,0:T(8,128)(2,1)}, bf16[2,3,2048,2304]{3,2,1,0:T(8,128)(2,1)}) custom-call(bf16[2048,896]{1,0:T(8,128)(2,1)} %bitcast.4, bf16[2048,896]{1,0:T(8,128)(2,1)} %bitcast.5, bf16[2,896,2304]{2,1,0:T(8,128)(2,1)} %refs_3_.1, bf16[2,896,2304]{2,1,0:T(8,128)(2,1)} %refs_6_.1, bf16[2,2304,896]{2,1,0:T(8,128)(2,1)} %refs_0_.1), custom_call_target="tpu_custom_call" | custom-call | flops 76101451776 | bytes 100000000 | tf_op jit(solution)/shard_map/rows/pallas_call | solution.py:200
  111.4 142.5 %scatter.1 = (bf16[3,2,128,128]{3,2,1,0:T(8,128)(2,1)}, f32[8,128]{1,0:T(8,128)}) custom-call(bf16[2,2,896,2048]{3,2,1,0:T(8,128)(2,1)} %get-tuple-element.24.xt_ref, bf16[2,3,2048,2304]{3,2,1,0:T(8,128)(2,1)} %get-tuple-element.25.ys_ref), custom_call_target="tpu_custom_call" | custom-call | flops 50734301184 | bytes 74317824 | tf_op jit(solution)/shard_map/scatter/pallas_call | solution.py:452
  253.9 109.0 %gather.1 = (bf16[3,2,4,4,8,128,128]{6,5,4,3,2,1,0:T(8,128)(2,1)}, f32[8,128]{1,0:T(8,128)}) custom-call(bf16[3,2,128,128]{3,2,1,0:T(8,128)(2,1)} %get-tuple-element.26.shard_ref, f32[8,128]{1,0:T(8,128)} %get-tuple-element.27.squares_ref), custom_call_target="tpu_custom_call" | custom-call | flops 2477260800 | bytes 49545216 | tf_op jit(solution)/shard_map/gather/pallas_call | solution.py:610
  362.9 89.3 %adamw.1 = (bf16[2,2304,896]{2,1,0:T(8,128)(2,1)}, f32[2,2304,896]{2,1,0:T(8,128)}, f32[2,2304,896]{2,1,0:T(8,128)}, bf16[2,896,2304]{2,1,0:T(8,128)(2,1)}, f32[...) custom-call(f32[8,128]{1,0:T(8,128)} %get-tuple-element.28.total_ref, ...), custom_call_target="tpu_custom_call" | custom-call | flops 371589120 | bytes 272498688 | tf_op jit(solution)/shard_map/adamw/pallas_call | solution.py:675

commit v3 on v1

--- a/solution.py
+++ b/solution.py
@@ -179,10 +179,11 @@
     need(("g", 0), ("u", 0))
 
     def panels(body):
-        lax.fori_loop(0, PANELS // 3, lambda i, carry: (body(3 * i), body(3 * i + 1), body(3 * i + 2), carry)[3], 0)
+        for p in range(PANELS):
+            body(p)
 
     def at(p):
-        return pl.ds(pl.multiple_of(p * PANEL, PANEL), PANEL)
+        return pl.ds(p * PANEL, PANEL)
 
     def forward0(p):
         gate, up = dot(a_buf[...], wg[0, :, at(p)]), dot(a_buf[...], wu[0, :, at(p)])
@@ -363,33 +364,15 @@
 
 
 SLOTS = (
-    ((2, 8, 5),),
-    ((2, 1, 6),),
-    ((1, 7, 1),),
-    (),
-    ((1, 8, 1), (1, 6, 2),),
-    ((2, 2, 6), (1, 3, 2),),
-    ((2, 6, 6),),
-    ((2, 0, 6), (1, 4, 2), (2, 5, 6), (2, 4, 6), (2, 7, 6),),
-    ((0, 1, 0), (0, 0, 0), (0, 2, 0), (1, 5, 2),),
-    ((1, 2, 3),),
-    ((1, 6, 3),),
-    ((1, 0, 4), (2, 8, 6), (2, 3, 6),),
-    (),
-    ((1, 7, 2), (0, 0, 1), (1, 1, 3), (1, 3, 3), (1, 8, 2),),
-    ((2, 1, 7), (0, 1, 1),),
-    ((0, 2, 1),),
-    ((2, 5, 7),),
-    ((0, 5, 0),),
-    ((1, 4, 3), (1, 5, 3),),
-    ((2, 4, 7),),
-    ((0, 3, 0),),
-    ((1, 6, 4), (0, 0, 2), (0, 4, 0),),
-    ((2, 2, 7), (1, 7, 3),),
-    (),
-    ((1, 8, 3),),
-    (),
-    ((2, 0, 7), (2, 6, 7), (2, 7, 7), (0, 8, 0), (0, 6, 0), (2, 8, 7), (1, 2, 4), (1, 6, 5), (0, 7, 0), (1, 4, 4), (1, 1, 4), (0, 1, 2), (0, 3, 1), (1, 5, 4), (1, 3, 4), (2, 3, 7), (1, 0, 5), (0, 5, 1), (2, 1, 8), (2, 5, 8), (1, 7, 4), (0, 2, 2), (1, 8, 4), (0, 6, 1), (2, 4, 8), (1, 1, 5), (1, 2, 5), (2, 0, 8), (2, 2, 8), (0, 4, 1), (2, 6, 8), (1, 5, 5), (2, 7, 8), (0, 0, 3), (1, 4, 5), (1, 3, 5), (2, 8, 8), (1, 7, 5), (2, 3, 8),),
+    ((2, 7, 5), (2, 8, 5), (2, 1, 6), (2, 4, 6), (1, 7, 1), (1, 3, 2),),
+    ((1, 6, 2), (1, 8, 1), (1, 4, 2), (2, 5, 6),),
+    ((0, 2, 0), (0, 1, 0), (0, 0, 0), (1, 0, 4), (2, 0, 6),),
+    ((2, 2, 6), (1, 3, 3), (2, 6, 6),),
+    ((1, 5, 2), (2, 7, 6), (1, 2, 3), (0, 0, 1), (1, 7, 2), (1, 1, 3), (2, 3, 6), (0, 1, 1),),
+    ((0, 5, 0), (0, 3, 0), (0, 2, 1),),
+    ((1, 6, 3), (1, 8, 2), (1, 5, 3), (0, 0, 2), (2, 8, 6), (1, 4, 3),),
+    ((1, 7, 3), (2, 4, 7), (0, 4, 0),),
+    ((1, 8, 3), (2, 1, 7), (2, 2, 7), (2, 5, 7), (2, 6, 7), (0, 8, 0), (1, 2, 4), (2, 0, 7), (1, 1, 4), (0, 6, 0), (1, 3, 4), (2, 7, 7), (1, 4, 4), (1, 6, 4), (1, 5, 4), (0, 7, 0), (2, 3, 7), (2, 8, 7), (0, 3, 1), (0, 5, 1), (2, 1, 8), (0, 1, 2), (2, 2, 8), (1, 0, 5), (1, 2, 5), (2, 5, 8), (1, 1, 5), (1, 7, 4), (1, 8, 4), (1, 4, 5), (2, 4, 8), (2, 0, 8), (1, 5, 5), (0, 4, 1), (2, 6, 8), (1, 6, 5), (0, 2, 2), (0, 6, 1), (1, 3, 5), (0, 0, 3), (2, 7, 8), (2, 3, 8), (2, 8, 8),),
     (),
 )
 
@@ -398,18 +381,21 @@
     recv, refs = refs[:27], refs[27:]
     xbuf, ybuf, x_sem, y_sem, send_sem, recv_sem = refs
     at = here()
-    total = 3 * PANELS
+    total = PANELS
 
     def load_x(g, kind):
         return pltpu.make_async_copy(xt_ref.at[g, kind], xbuf.at[kind], x_sem.at[kind])
 
     def load_y(g, n):
-        lanes = pl.ds(pl.multiple_of((n % PANELS) * PANEL, PANEL), PANEL)
-        return pltpu.make_async_copy(ys_ref.at[g, n // PANELS, :, lanes], ybuf.at[n % 3], y_sem.at[n % 3])
+        copies = []
+        for q in range(3):
+            lanes = pl.ds(pl.multiple_of((n % 3) * (3 * PANEL) + q * PANEL, PANEL), PANEL)
+            copies.append(pltpu.make_async_copy(ys_ref.at[g, n // 3, :, lanes], ybuf.at[(g + n) % 2, q], y_sem.at[(g + n) % 2, q]))
+        return copies
 
     load_x(0, 0).start()
-    load_y(0, 0).start()
-    load_y(0, 1).start()
+    for one in load_y(0, 0):
+        one.start()
     load_x(0, 1).start()
     squares_ref[...] = jnp.zeros_like(squares_ref)
     for g in range(2):
@@ -432,14 +418,19 @@
         def slot(n, carry):
             @pl.when(jnp.logical_and(n < total, i < 2))
             def _():
-                j, p = n // PANELS, n % PANELS
+                j = n // 3
                 kind = jnp.minimum(j, 1)
+
+                @pl.when(n + 1 < total)
+                def _():
+                    for one in load_y(i, n + 1):
+                        one.start()
 
                 @pl.when(n == 0)
                 def _():
                     load_x(i, 0).wait()
 
-                @pl.when(n == PANELS)
+                @pl.when(n == 3)
                 def _():
                     load_x(i, 1).wait()
 
@@ -447,26 +438,21 @@
                     def _():
                         load_x(i + 1, 0).start()
 
-                load_y(i, n).wait()
-
-                @pl.when(n + 2 < total)
-                def _():
-                    load_y(i, n + 2).start()
-
-                @pl.when(jnp.logical_and(n + 2 >= total, i < 1))
-                def _():
-                    load_y(i + 1, n + 2 - total).start()
-
-                out = dot(xbuf[kind], ybuf[n % 3])
-                for half in range(PANEL // LANES):
-                    for b in range(D // SHARD):
-                        d = (2 * p + half) * (D // SHARD) + b
-                        block = out[b * SHARD : (b + 1) * SHARD, half * LANES : (half + 1) * LANES]
-                        own[i, j, d // 32, (d // 8) % 4, d % 8] = block.astype(BF)
+                for one in load_y(i, n):
+                    one.wait()
+                for q in range(3):
+                    out = dot(xbuf[kind], ybuf[(i + n) % 2, q])
+                    for half in range(PANEL // LANES):
+                        for b in range(D // SHARD):
+                            d = (2 * (3 * (n % 3) + q) + half) * (D // SHARD) + b
+                            block = out[b * SHARD : (b + 1) * SHARD, half * LANES : (half + 1) * LANES]
+                            own[i, j, d // 32, (d // 8) % 4, d % 8] = block.astype(BF)
 
                 @pl.when(jnp.logical_and(n == total - 1, i < 1))
                 def _():
                     load_x(i + 1, 1).start()
+                    for one in load_y(i + 1, 0):
+                        one.start()
 
             def serve(todo):
                 for late, key, which in todo:
@@ -505,9 +491,9 @@
             pltpu.VMEM((2, 3, 4, 4, 8, SHARD, LANES), BF),
             *recv_shapes(),
             pltpu.VMEM((2, D, TOKENS), BF),
-            pltpu.VMEM((3, TOKENS, PANEL), BF),
+            pltpu.VMEM((2, 3, TOKENS, PANEL), BF),
             pltpu.SemaphoreType.DMA((2,)),
-            pltpu.SemaphoreType.DMA((3,)),
+            pltpu.SemaphoreType.DMA((2, 3)),
             pltpu.SemaphoreType.DMA((2, 3, 3, 2)),
             pltpu.SemaphoreType.DMA((2, 3, 3, 8, 2)),
         ],

time: 460 us -> 439 us (0.954)
  Pallas kernels: 459 us -> 438 us
    pallas_call x1, Pallas kernels: 149 us -> 135 us  [scattered(): pl.pallas_call(scatter_kernel, out_shape=(jax.ShapeDtypeStruct((3, 2, SHA...]
    pallas_call x1, Pallas kernels: 118 us -> 111 us  [row_wise(): pl.pallas_call(rows_kernel, grid=(tokens // TB,), out_shape=(jax.ShapeDty...]
where the time goes in v3:
time: 439 us
  Pallas kernels  438 us (100%)
    pallas_call x1, Pallas kernels, scattered(): pl.pallas_call(scatter_kernel, out_shape=(jax.ShapeDtypeStruct((3, 2, SHA...  135 us
    pallas_call x1, Pallas kernels, row_wise(): pl.pallas_call(rows_kernel, grid=(tokens // TB,), out_shape=(jax.ShapeDty...  111 us
    pallas_call x1, Pallas kernels, gathered(): pl.pallas_call(gather_kernel, out_shape=(jax.ShapeDtypeStruct((3, 2, 4, 4...  103 us
    pallas_call x1, Pallas kernels, adamw(): pl.pallas_call(adamw_kernel, grid=(2, PANELS), out_shape=[jax.ShapeDtypeS...  89.3 us

profile of v3, /device:TPU:2, one launch (start us, length us, event | category | flops | bytes accessed | tf_op | source)
XLA Modules:
  0.0 439.0 jit_solution(7921731458303520409)
XLA Ops:
  0.6 110.7 %rows.1 = (bf16[2,2,896,2048]{3,2,1,0:T(8,128)(2,1)}, bf16[2,3,2048,2304]{3,2,1,0:T(8,128)(2,1)}) custom-call(bf16[2048,896]{1,0:T(8,128)(2,1)} %bitcast.4, bf16[2048,896]{1,0:T(8,128)(2,1)} %bitcast.5, bf16[2,896,2304]{2,1,0:T(8,128)(2,1)} %refs_3_.1, bf16[2,896,2304]{2,1,0:T(8,128)(2,1)} %refs_6_.1, bf16[2,2304,896]{2,1,0:T(8,128)(2,1)} %refs_0_.1), custom_call_target="tpu_custom_call" | custom-call | flops 76101451776 | bytes 100000000 | tf_op jit(solution)/shard_map/rows/pallas_call | solution.py:252
  111.4 134.9 %scatter.1 = (bf16[3,2,128,128]{3,2,1,0:T(8,128)(2,1)}, f32[8,128]{1,0:T(8,128)}) custom-call(bf16[2,2,896,2048]{3,2,1,0:T(8,128)(2,1)} %get-tuple-element.24.xt_ref, bf16[2,3,2048,2304]{3,2,1,0:T(8,128)(2,1)} %get-tuple-element.25.ys_ref), custom_call_target="tpu_custom_call" | custom-call | flops 50734301184 | bytes 74317824 | tf_op jit(solution)/shard_map/scatter/pallas_call | solution.py:485
  246.3 103.2 %gather.1 = (bf16[3,2,4,4,8,128,128]{6,5,4,3,2,1,0:T(8,128)(2,1)}, f32[8,128]{1,0:T(8,128)}) custom-call(bf16[3,2,128,128]{3,2,1,0:T(8,128)(2,1)} %get-tuple-element.26.shard_ref, f32[8,128]{1,0:T(8,128)} %get-tuple-element.27.squares_ref), custom_call_target="tpu_custom_call" | custom-call | flops 2477260800 | bytes 49545216 | tf_op jit(solution)/shard_map/gather/pallas_call | solution.py:638
  349.5 89.3 %adamw.1 = (bf16[2,2304,896]{2,1,0:T(8,128)(2,1)}, f32[2,2304,896]{2,1,0:T(8,128)}, f32[2,2304,896]{2,1,0:T(8,128)}, bf16[2,896,2304]{2,1,0:T(8,128)(2,1)}, f32[...) custom-call(f32[8,128]{1,0:T(8,128)} %get-tuple-element.28.total_ref, ...), custom_call_target="tpu_custom_call" | custom-call | flops 371589120 | bytes 272498688 | tf_op jit(solution)/shard_map/adamw/pallas_call | solution.py:703

commit v4 on v3

--- a/solution.py
+++ b/solution.py
@@ -129,7 +129,7 @@
     return lax.dot_general(a, b, (((1,), (1,)), ((), ())), preferred_element_type=F32)
 
 
-def rows_kernel(x_ref, dy_ref, wg_ref, wu_ref, wd_ref, xt_hbm, ys_hbm, wg, wu, wd, gate0, up0, a_buf, h_buf, xt_ref, ys_ref, load_sem, xt_sem, ys_sem):
+def rows_kernel(x_ref, dy_ref, wg_ref, wu_ref, wd_ref, xt_hbm, ys_hbm, wg, wu, wd, gate0, up0, a_buf, h_buf, xt_ref, ys_ref, load_sem, xt_sem, ys_sem, late_sem):
     block = pl.program_id(0)
     first, last = block == 0, block == pl.num_programs(0) - 1
     loads = {
@@ -157,6 +157,12 @@
 
     def ys_out(*at):
         return pltpu.make_async_copy(ys_ref.at[at], ys_hbm.at[(*at, tokens, slice(None))], ys_sem.at[at])
+
+    def late_out(j, third):
+        lanes = pl.ds(third * 3 * PANEL, 3 * PANEL)
+        return pltpu.make_async_copy(ys_ref.at[1, j, :, lanes], ys_hbm.at[1, j, tokens, lanes], late_sem.at[j - 1, third])
+
+    late_outs = [late_out(j, third) for j in (1, 2) for third in range(3)]
 
     def free(*outs):
         @pl.when(jnp.logical_not(first))
@@ -225,26 +231,27 @@
     dh = scale * da - h * (scale * scale * scale * jnp.mean(da * h, -1, keepdims=True))
     dh = (dy_ref[...].astype(F32) + dh.astype(BF).astype(F32)).astype(BF)
     a_buf[...] = dh
-    free(xt_out(1, 0))
+    free(xt_out(1, 0), *late_outs)
     xt_ref[1, 0] = dh.T
     xt_out(1, 0).start()
-    free(ys_out(1, 1), ys_out(1, 2))
 
     def back0(p):
         d = dot_t(a_buf[...], wd[0, at(p), :])
         ys_ref[1, 1, :, at(p)], ys_ref[1, 2, :, at(p)], _ = back(d, gate0[:, at(p)], up0[:, at(p)])
 
-    panels(back0)
-    for j in (1, 2):
-        ys_out(1, j).start()
+    for p in range(PANELS):
+        back0(p)
+        if (p + 1) % 3 == 0:
+            for j in (1, 2):
+                late_out(j, p // 3).start()
 
     @pl.when(last)
     def _():
         for g in range(2):
             for kind in range(2):
                 xt_out(g, kind).wait()
-            for j in range(3):
-                ys_out(g, j).wait()
+        for one in (ys_out(0, 0), ys_out(0, 1), ys_out(0, 2), ys_out(1, 0), *late_outs):
+            one.wait()
 
 
 def row_wise(x, dy, w_gate, w_up, w_down):
@@ -267,6 +274,7 @@
             pltpu.VMEM((2, 3, TB, FF), BF),
             pltpu.SemaphoreType.DMA((3, 2)),
             pltpu.SemaphoreType.DMA((2, 2)),
+            pltpu.SemaphoreType.DMA((2, 3)),
             pltpu.SemaphoreType.DMA((2, 3)),
         ],
         compiler_params=pltpu.CompilerParams(vmem_limit_bytes=LIMIT, dimension_semantics=("arbitrary",)),
@@ -616,8 +624,10 @@
     events = gather_order(streams)
     actions = {(j, c): gather_actions(j, c, at, full, send_sem, recv_sem) for j, c in streams}
     count = dict.fromkeys(streams, 0)
-    left = {j: 3 for j in range(3)}
-    outs = [pltpu.make_async_copy(full.at[j], out_ref.at[j], out_sem.at[j]) for j in range(3)]
+    outs = {}
+    for j, c in streams:
+        place = (j, slice(None), *place_of({}, None, *colour(j, c)))
+        outs[j, c] = pltpu.make_async_copy(full.at[place], out_ref.at[place], out_sem.at[j, c])
     summed = 1
     for t, key in events:
         while summed < len(sums) and t > 5.0 * summed:
@@ -626,10 +636,8 @@
         actions[key][count[key]]()
         count[key] += 1
         if count[key] == len(actions[key]):
-            left[key[0]] -= 1
-            if left[key[0]] == 0:
-                outs[key[0]].start()
-    for one in outs:
+            outs[key].start()
+    for one in outs.values():
         one.wait()
 
 
@@ -646,7 +654,7 @@
             pltpu.VMEM((4, 8, LANES), F32),
             pltpu.VMEM((8, 8, LANES), F32),
             pltpu.SemaphoreType.DMA,
-            pltpu.SemaphoreType.DMA((3,)),
+            pltpu.SemaphoreType.DMA((3, 3)),
             pltpu.SemaphoreType.DMA((3, 3, 2)),
             pltpu.SemaphoreType.DMA((3, 3, 8, 2)),
             pltpu.SemaphoreType.DMA((13,)),
@@ -658,10 +666,13 @@
     )(shards, squares)
 
 
-def adamw_kernel(total_ref, g_ref, *refs):
+HALF = D // 2
+
+
+def adamw_kernel(total_ref, down_g, gate_g0, gate_g1, up_g0, up_g1, *refs):
     ins, outs, factor_ref = refs[:9], refs[9:18], refs[18]
 
-    @pl.when(jnp.logical_and(pl.program_id(0) == 0, pl.program_id(1) == 0))
+    @pl.when(pl.program_id(0) + pl.program_id(1) + pl.program_id(2) == 0)
     def _():
         mean = jnp.sum(total_ref[...], keepdims=True) * (1.0 / (6 * D * FF))
         factor_ref[...] = jnp.broadcast_to(jnp.minimum(1.0, 0.5 * lax.rsqrt(mean + 1e-30)), factor_ref.shape)
@@ -679,42 +690,49 @@
         mo_ref[place] = m
         vo_ref[place] = v
 
-    for half in range(PANEL // LANES):
+    for half, gs in enumerate(((gate_g0, up_g0), (gate_g1, up_g1))):
         lanes = pl.ds(half * LANES, LANES)
 
         def body(i, carry):
-            here_rows = pl.ds(pl.multiple_of(half * D + i * 128, 128), 128)
-            rows = pl.ds(pl.multiple_of(i * 128, 128), 128)
-            for j in (1, 2):
-                one(j, g_ref[j, here_rows, :].astype(F32) * factor, (rows, lanes))
+            rows = pl.ds(pl.multiple_of(i * 64, 64), 64)
+            for j, g_ref in zip((1, 2), gs, strict=True):
+                one(j, g_ref[rows, :].astype(F32) * factor, (rows, lanes))
             return carry
 
-        lax.fori_loop(0, D // 128, body, 0)
-        for i in range(D // 128):
-            g = g_ref[0, pl.ds(half * D + i * 128, 128), :].astype(F32) * factor
-            one(0, g.T, (lanes, pl.ds(i * 128, 128)))
+        lax.fori_loop(0, HALF // 64, body, 0)
+    for i in range(D // 128):
+        g = down_g[pl.ds(i * 128, 128), :].astype(F32) * factor
+        one(0, g.T, (slice(None), pl.ds(i * 128, 128)))
 
 
 def adamw(total, g, weights):
-    wide = pl.BlockSpec((None, D, PANEL), lambda l, p: (l, 0, p))
-    tall = pl.BlockSpec((None, PANEL, D), lambda l, p: (l, p, 0))
+    wide = pl.BlockSpec((None, HALF, PANEL), lambda l, p, r: (l, r, p))
+    tall = pl.BlockSpec((None, LANES, D), lambda l, p, r: (l, 2 * p + r, 0))
     specs = [tall] * 3 + [wide] * 6
     arrays = [a for one in weights for a in one]
+
+    def part(j, half):
+        return pl.BlockSpec((None, None, HALF, LANES), lambda l, p, r: (j, 1 - l, 4 * p + 2 * half + r, 0))
+
     return pl.pallas_call(
         adamw_kernel,
-        grid=(2, PANELS),
+        grid=(2, PANELS, 2),
         out_shape=[jax.ShapeDtypeStruct(a.shape, a.dtype) for a in arrays],
         in_specs=[
-            pl.BlockSpec((8, LANES), lambda l, p: (0, 0)),
-            pl.BlockSpec((3, None, PANEL // LANES * D, LANES), lambda l, p: (0, 1 - l, p, 0)),
+            pl.BlockSpec((8, LANES), lambda l, p, r: (0, 0)),
+            pl.BlockSpec((None, None, D, LANES), lambda l, p, r: (0, 1 - l, 2 * p + r, 0)),
+            part(1, 0),
+            part(1, 1),
+            part(2, 0),
+            part(2, 1),
             *specs,
         ],
         out_specs=specs,
         scratch_shapes=[pltpu.VMEM((8, LANES), F32)],
-        compiler_params=pltpu.CompilerParams(vmem_limit_bytes=LIMIT, dimension_semantics=("arbitrary", "arbitrary")),
+        compiler_params=pltpu.CompilerParams(vmem_limit_bytes=LIMIT, dimension_semantics=("arbitrary",) * 3),
         cost_estimate=pl.CostEstimate(flops=6 * D * FF * 30, bytes_accessed=6 * D * FF * 22, transcendentals=6 * D * FF),
         name="adamw",
-    )(total, g, *arrays)
+    )(total, g, g, g, g, g, *arrays)
 
 
 def solution(mesh):

time: 439 us -> 446 us (1.016)
  Pallas kernels: 438 us -> 445 us
    pallas_call x1, Pallas kernels: 89.3 us -> 98.8 us  [adamw(): pl.pallas_call(adamw_kernel, grid=(2, PANELS, 2), out_shape=[jax.ShapeDty...]
where the time goes in v4:
time: 446 us
  Pallas kernels  445 us (100%)
    pallas_call x1, Pallas kernels, scattered(): pl.pallas_call(scatter_kernel, out_shape=(jax.ShapeDtypeStruct((3, 2, SHA...  135 us
    pallas_call x1, Pallas kernels, row_wise(): pl.pallas_call(rows_kernel, grid=(tokens // TB,), out_shape=(jax.ShapeDty...  109 us
    pallas_call x1, Pallas kernels, gathered(): pl.pallas_call(gather_kernel, out_shape=(jax.ShapeDtypeStruct((3, 2, 4, 4...  102 us
    pallas_call x1, Pallas kernels, adamw(): pl.pallas_call(adamw_kernel, grid=(2, PANELS, 2), out_shape=[jax.ShapeDty...  98.8 us

profile of v4, /device:TPU:2, one launch (start us, length us, event | category | flops | bytes accessed | tf_op | source)
XLA Modules:
  0.0 446.0 jit_solution(10548344984042441499)
XLA Ops:
  0.6 109.0 %rows.1 = (bf16[2,2,896,2048]{3,2,1,0:T(8,128)(2,1)}, bf16[2,3,2048,2304]{3,2,1,0:T(8,128)(2,1)}) custom-call(bf16[2048,896]{1,0:T(8,128)(2,1)} %bitcast.8, bf16[2048,896]{1,0:T(8,128)(2,1)} %bitcast.9, bf16[2,896,2304]{2,1,0:T(8,128)(2,1)} %refs_3_.1, bf16[2,896,2304]{2,1,0:T(8,128)(2,1)} %refs_6_.1, bf16[2,2304,896]{2,1,0:T(8,128)(2,1)} %refs_0_.1), custom_call_target="tpu_custom_call" | custom-call | flops 76101451776 | bytes 100000000 | tf_op jit(solution)/shard_map/rows/pallas_call | solution.py:259
  109.7 134.9 %scatter.1 = (bf16[3,2,128,128]{3,2,1,0:T(8,128)(2,1)}, f32[8,128]{1,0:T(8,128)}) custom-call(bf16[2,2,896,2048]{3,2,1,0:T(8,128)(2,1)} %get-tuple-element.24.xt_ref, bf16[2,3,2048,2304]{3,2,1,0:T(8,128)(2,1)} %get-tuple-element.25.ys_ref), custom_call_target="tpu_custom_call" | custom-call | flops 50734301184 | bytes 74317824 | tf_op jit(solution)/shard_map/scatter/pallas_call | solution.py:493
  244.5 102.4 %gather.1 = (bf16[3,2,4,4,8,128,128]{6,5,4,3,2,1,0:T(8,128)(2,1)}, f32[8,128]{1,0:T(8,128)}) custom-call(bf16[3,2,128,128]{3,2,1,0:T(8,128)(2,1)} %get-tuple-element.26.shard_ref, f32[8,128]{1,0:T(8,128)} %get-tuple-element.27.squares_ref), custom_call_target="tpu_custom_call" | custom-call | flops 2477260800 | bytes 49545216 | tf_op jit(solution)/shard_map/gather/pallas_call | solution.py:646
  347.0 98.8 %adamw.1 = (bf16[2,2304,896]{2,1,0:T(8,128)(2,1)}, f32[2,2304,896]{2,1,0:T(8,128)}, f32[2,2304,896]{2,1,0:T(8,128)}, bf16[2,896,2304]{2,1,0:T(8,128)(2,1)}, f32[...) custom-call(f32[8,128]{1,0:T(8,128)} %get-tuple-element.28.total_ref, ...), custom_call_target="tpu_custom_call" | custom-call | flops 371589120 | bytes 272498688 | tf_op jit(solution)/shard_map/adamw/pallas_call | solution.py:717

commit v5 on v3

--- a/solution.py
+++ b/solution.py
@@ -129,7 +129,7 @@
     return lax.dot_general(a, b, (((1,), (1,)), ((), ())), preferred_element_type=F32)
 
 
-def rows_kernel(x_ref, dy_ref, wg_ref, wu_ref, wd_ref, xt_hbm, ys_hbm, wg, wu, wd, gate0, up0, a_buf, h_buf, xt_ref, ys_ref, load_sem, xt_sem, ys_sem):
+def rows_kernel(x_ref, dy_ref, wg_ref, wu_ref, wd_ref, xt_hbm, ys_hbm, wg, wu, wd, gate0, up0, a_buf, h_buf, xt_ref, ys_ref, load_sem, xt_sem, ys_sem, late_sem):
     block = pl.program_id(0)
     first, last = block == 0, block == pl.num_programs(0) - 1
     loads = {
@@ -157,6 +157,12 @@
 
     def ys_out(*at):
         return pltpu.make_async_copy(ys_ref.at[at], ys_hbm.at[(*at, tokens, slice(None))], ys_sem.at[at])
+
+    def late_out(j, third):
+        lanes = pl.ds(third * 3 * PANEL, 3 * PANEL)
+        return pltpu.make_async_copy(ys_ref.at[1, j, :, lanes], ys_hbm.at[1, j, tokens, lanes], late_sem.at[j - 1, third])
+
+    late_outs = [late_out(j, third) for j in (1, 2) for third in range(3)]
 
     def free(*outs):
         @pl.when(jnp.logical_not(first))
@@ -225,26 +231,27 @@
     dh = scale * da - h * (scale * scale * scale * jnp.mean(da * h, -1, keepdims=True))
     dh = (dy_ref[...].astype(F32) + dh.astype(BF).astype(F32)).astype(BF)
     a_buf[...] = dh
-    free(xt_out(1, 0))
+    free(xt_out(1, 0), *late_outs)
     xt_ref[1, 0] = dh.T
     xt_out(1, 0).start()
-    free(ys_out(1, 1), ys_out(1, 2))
 
     def back0(p):
         d = dot_t(a_buf[...], wd[0, at(p), :])
         ys_ref[1, 1, :, at(p)], ys_ref[1, 2, :, at(p)], _ = back(d, gate0[:, at(p)], up0[:, at(p)])
 
-    panels(back0)
-    for j in (1, 2):
-        ys_out(1, j).start()
+    for p in range(PANELS):
+        back0(p)
+        if (p + 1) % 3 == 0:
+            for j in (1, 2):
+                late_out(j, p // 3).start()
 
     @pl.when(last)
     def _():
         for g in range(2):
             for kind in range(2):
                 xt_out(g, kind).wait()
-            for j in range(3):
-                ys_out(g, j).wait()
+        for one in (ys_out(0, 0), ys_out(0, 1), ys_out(0, 2), ys_out(1, 0), *late_outs):
+            one.wait()
 
 
 def row_wise(x, dy, w_gate, w_up, w_down):
@@ -267,6 +274,7 @@
             pltpu.VMEM((2, 3, TB, FF), BF),
             pltpu.SemaphoreType.DMA((3, 2)),
             pltpu.SemaphoreType.DMA((2, 2)),
+            pltpu.SemaphoreType.DMA((2, 3)),
             pltpu.SemaphoreType.DMA((2, 3)),
         ],
         compiler_params=pltpu.CompilerParams(vmem_limit_bytes=LIMIT, dimension_semantics=("arbitrary",)),
@@ -616,8 +624,10 @@
     events = gather_order(streams)
     actions = {(j, c): gather_actions(j, c, at, full, send_sem, recv_sem) for j, c in streams}
     count = dict.fromkeys(streams, 0)
-    left = {j: 3 for j in range(3)}
-    outs = [pltpu.make_async_copy(full.at[j], out_ref.at[j], out_sem.at[j]) for j in range(3)]
+    outs = {}
+    for j, c in streams:
+        place = (j, slice(None), *place_of({}, None, *colour(j, c)))
+        outs[j, c] = pltpu.make_async_copy(full.at[place], out_ref.at[place], out_sem.at[j, c])
     summed = 1
     for t, key in events:
         while summed < len(sums) and t > 5.0 * summed:
@@ -626,10 +636,8 @@
         actions[key][count[key]]()
         count[key] += 1
         if count[key] == len(actions[key]):
-            left[key[0]] -= 1
-            if left[key[0]] == 0:
-                outs[key[0]].start()
-    for one in outs:
+            outs[key].start()
+    for one in outs.values():
         one.wait()
 
 
@@ -646,7 +654,7 @@
             pltpu.VMEM((4, 8, LANES), F32),
             pltpu.VMEM((8, 8, LANES), F32),
             pltpu.SemaphoreType.DMA,
-            pltpu.SemaphoreType.DMA((3,)),
+            pltpu.SemaphoreType.DMA((3, 3)),
             pltpu.SemaphoreType.DMA((3, 3, 2)),
             pltpu.SemaphoreType.DMA((3, 3, 8, 2)),
             pltpu.SemaphoreType.DMA((13,)),

time: 439 us -> 437 us (level)
  no operation moved by 1% of the time
where the time goes in v5:
time: 437 us; the launch traced here: 436 us
  Pallas kernels  436 us (100%)
    pallas_call x1, Pallas kernels, scattered(): pl.pallas_call(scatter_kernel, out_shape=(jax.ShapeDtypeStruct((3, 2, SHA...  135 us
    pallas_call x1, Pallas kernels, row_wise(): pl.pallas_call(rows_kernel, grid=(tokens // TB,), out_shape=(jax.ShapeDty...  109 us
    pallas_call x1, Pallas kernels, gathered(): pl.pallas_call(gather_kernel, out_shape=(jax.ShapeDtypeStruct((3, 2, 4, 4...  102 us
    pallas_call x1, Pallas kernels, adamw(): pl.pallas_call(adamw_kernel, grid=(2, PANELS), out_shape=[jax.ShapeDtypeS...  89.3 us

profile of v5, /device:TPU:2, one launch (start us, length us, event | category | flops | bytes accessed | tf_op | source)
XLA Modules:
  0.0 436.4 jit_solution(17459122691419019438)
XLA Ops:
  0.6 109.0 %rows.1 = (bf16[2,2,896,2048]{3,2,1,0:T(8,128)(2,1)}, bf16[2,3,2048,2304]{3,2,1,0:T(8,128)(2,1)}) custom-call(bf16[2048,896]{1,0:T(8,128)(2,1)} %bitcast.4, bf16[2048,896]{1,0:T(8,128)(2,1)} %bitcast.5, bf16[2,896,2304]{2,1,0:T(8,128)(2,1)} %refs_3_.1, bf16[2,896,2304]{2,1,0:T(8,128)(2,1)} %refs_6_.1, bf16[2,2304,896]{2,1,0:T(8,128)(2,1)} %refs_0_.1), custom_call_target="tpu_custom_call" | custom-call | flops 76101451776 | bytes 100000000 | tf_op jit(solution)/shard_map/rows/pallas_call | solution.py:259
  109.7 134.9 %scatter.1 = (bf16[3,2,128,128]{3,2,1,0:T(8,128)(2,1)}, f32[8,128]{1,0:T(8,128)}) custom-call(bf16[2,2,896,2048]{3,2,1,0:T(8,128)(2,1)} %get-tuple-element.24.xt_ref, bf16[2,3,2048,2304]{3,2,1,0:T(8,128)(2,1)} %get-tuple-element.25.ys_ref), custom_call_target="tpu_custom_call" | custom-call | flops 50734301184 | bytes 74317824 | tf_op jit(solution)/shard_map/scatter/pallas_call | solution.py:493
  244.5 102.4 %gather.1 = (bf16[3,2,4,4,8,128,128]{6,5,4,3,2,1,0:T(8,128)(2,1)}, f32[8,128]{1,0:T(8,128)}) custom-call(bf16[3,2,128,128]{3,2,1,0:T(8,128)(2,1)} %get-tuple-element.26.shard_ref, f32[8,128]{1,0:T(8,128)} %get-tuple-element.27.squares_ref), custom_call_target="tpu_custom_call" | custom-call | flops 2477260800 | bytes 49545216 | tf_op jit(solution)/shard_map/gather/pallas_call | solution.py:646
  347.0 89.3 %adamw.1 = (bf16[2,2304,896]{2,1,0:T(8,128)(2,1)}, f32[2,2304,896]{2,1,0:T(8,128)}, f32[2,2304,896]{2,1,0:T(8,128)}, bf16[2,896,2304]{2,1,0:T(8,128)(2,1)}, f32[...) custom-call(f32[8,128]{1,0:T(8,128)} %get-tuple-element.28.total_ref, ...), custom_call_target="tpu_custom_call" | custom-call | flops 371589120 | bytes 272498688 | tf_op jit(solution)/shard_map/adamw/pallas_call | solution.py:711
